TPU v7x, 32 devices: a whole 2x2x4 slice. The times are simulated.
32 devices in a mesh: blk: 32 (over z, y, x, core).
Axes of the slice: x: 2, y: 2, z: 4, core: 2. Of those that a mesh axis runs over, the one named last changes fastest.
Arguments:
- panel_left: bfloat16 [64, 64, 2048], P('blk'), may hold values from -0.75 to 0.75
- panel_right: bfloat16 [64, 64, 2048], P('blk'), may hold values from -0.125 to 0.125
- ranks: int32 [64], P('blk'), may hold values from 1 to 64
- rhs: float32 [64, 64, 2048], P('blk'), may hold values from -6 to 6
- pivot_left: bfloat16 [2048, 64], P('blk'), may hold values from -0.75 to 0.75
- pivot_right: bfloat16 [2048, 64], P('blk'), may hold values from -6 to 6
- finished: float32 [2048, 64], P('blk'), may hold values from -6 to 6
- pivot_rhs: float32 [2048, 64], P('blk'), may hold values from -6 to 6
- diag_inverse: float32 [2048, 2048], P('blk'), as said below
Outputs:
- new_left: bfloat16 [64, 64, 2048], P('blk')
- new_rhs: float32 [64, 64, 2048], P('blk')
- next_solution: float32 [2048, 64], P('blk')
Inputs may be any that keep to these rules, and one draw needn't show every extreme that they name: diag_inverse is lower triangular with diagonal entries between 1 and 2.
All inputs are finite; a program needn't handle non-finite values.
Results may differ from a plain program's by a relative error of at most 0.0049.
Values sent between devices are 32-bit elements; how exact they have to be, the bound alone decides.
No kernel may reach another device: no remote copies, remote signals or barrier semaphores. Data moves between devices by JAX's collectives and lax.ppermute only.
A program may use at most 64 MiB of HBM per device.

v0:
```python
import jax
import jax.numpy as jnp
from jax import lax
from jax.sharding import PartitionSpec as P

HIGH = lax.Precision.HIGHEST


def shards(
    panel_left, panel_right, ranks, rhs, pivot_left, pivot_right, finished, pivot_rhs, diag_inverse
):
    kmax = panel_left.shape[1]
    mask = (jnp.arange(kmax, dtype=jnp.int32)[None, :] < ranks[:, None]).astype(jnp.bfloat16)
    left_m = panel_left * mask[:, :, None]
    right_wide = (panel_right * mask[:, :, None]).astype(jnp.float32)
    pivot_wide = pivot_right.astype(jnp.float32)
    right_piece = lax.all_gather(pivot_wide, "blk", axis=0, tiled=True)
    solved_piece = lax.all_gather(finished, "blk", axis=0, tiled=True)
    gram_sum = jnp.einsum("rkn,nj->rkj", right_wide, right_piece, precision=HIGH)
    proj_sum = jnp.einsum("rkn,nj->rkj", right_wide, solved_piece, precision=HIGH)
    pivot_sum = jnp.dot(right_piece.T, solved_piece, precision=HIGH)
    new_left = jnp.einsum(
        "rkj,rkn->rjn", gram_sum.astype(jnp.bfloat16), left_m, preferred_element_type=jnp.float32
    ).astype(jnp.bfloat16)
    new_rhs = rhs - jnp.einsum("rkj,rkn->rjn", proj_sum, left_m.astype(jnp.float32), precision=HIGH)
    pivot_new = pivot_rhs - jnp.dot(pivot_left.astype(jnp.float32), pivot_sum, precision=HIGH)
    next_solution = jnp.dot(
        diag_inverse, lax.all_gather(pivot_new, "blk", axis=0, tiled=True), precision=HIGH
    )
    return (new_left, new_rhs, next_solution)


def solution(mesh):
    in_specs = (
        P("blk", None, None),
        P("blk", None, None),
        P("blk"),
        P("blk", None, None),
        P("blk", None),
        P("blk", None),
        P("blk", None),
        P("blk", None),
        P("blk", None),
    )
    out_specs = (P("blk", None, None), P("blk", None, None), P("blk", None))
    return jax.shard_map(shards, mesh=mesh, in_specs=in_specs, out_specs=out_specs, check_vma=False)
```

profile of v0, /device:TPU:0, one launch (start us, length us, event | category | flops | bytes accessed | tf_op | source)
XLA Modules:
  0.0 138.4 jit_solution(10801241229913180033)
XLA Ops:
  0.6 0.0 copy-start
  0.6 0.8 compare_convert_fusion
  1.4 0.7 convert_element_type.20
  2.2 0.0 copy-start.1
  2.2 46.3 %all_gather.9 = f32[2048,64]{1,0:T(8,128)S(1)} all-gather(f32[64,64]{1,0:T(8,128)S(1)} %convert_element_type.20), channel_id=1, replica_groups=mesh['blk'=32] {'blk'}, dimensions={0}, use_global_device_ids=true | all-gather | bytes 540672 | tf_op jit(solution)/shard_map/all_gather | solution.py:17
  48.5 0.0 copy-done.1
  48.5 0.0 copy-start.2
  48.5 1.1 convolution_convert_fusion.1
  49.5 0.0 copy-done.2
  49.5 0.0 copy-start.4
  49.5 1.1 convolution_convert_fusion
  50.7 0.0 copy-done.4
  50.7 39.5 %all_gather.10 = f32[2048,64]{1,0:T(8,128)S(1)} all-gather(f32[64,64]{1,0:T(8,128)S(1)} %copy-done.4), channel_id=1, replica_groups=mesh['blk'=32] {'blk'}, dimensions={0}, use_global_device_ids=true | all-gather | bytes 540672 | tf_op jit(solution)/shard_map/all_gather | solution.py:18
  90.2 1.9 %fusion.12 = f32[64,64]{1,0:T(8,128)S(1)} fusion(f32[2048,64]{1,0:T(8,128)S(1)} %all_gather.9, f32[2048,64]{1,0:T(8,128)S(1)} %all_gather.10), kind=kOutput, calls=%fused_computation.18 | convolution fusion | flops 100663296 | bytes 1064960 | tf_op jit(solution)/shard_map/dot_general | solution.py:21
  92.1 0.0 copy-start.5
  92.1 0.0 copy-start.6
  92.1 0.0 copy-start.3
  92.1 1.1 fusion.1
  93.2 0.0 copy-done.5
  93.2 0.0 copy-done.6
  93.2 0.1 fusion
  93.3 0.0 copy-done.3
  93.3 1.6 %convolution_subtract_fusion = f32[2,64,2048]{2,1,0:T(8,128)} fusion(f32[2,64,2048]{2,1,0:T(8,128)S(1)} %copy-done.3, f32[2,64,64]{1,2,0:T(8,128)S(1)} %fusion.1, bf16[2,64,2048]{2,1,0:T(8,128)(2,1)S(1)} %copy-done.2, bf16[2,64]{1,0:T(2,128)(2,1)S(1)} %compare_convert_fusion), kind=kOutput, calls=%fused_computation | convolution fusion | flops 201850880 | bytes 2654464 | tf_op jit(solution)/shard_map/rkj,rkn->rjn/dot_general | solution.py:25
  95.0 40.9 %all_gather.11 = f32[2048,64]{1,0:T(8,128)S(1)} all-gather(f32[64,64]{1,0:T(8,128)S(1)} %fusion), channel_id=1, replica_groups=mesh['blk'=32] {'blk'}, dimensions={0}, use_global_device_ids=true | all-gather | bytes 540672 | tf_op jit(solution)/shard_map/all_gather | solution.py:28
  135.8 0.0 copy-done
  135.9 1.8 %convolution_bitcast_fusion = f32[64,64]{0,1:T(8,128)S(1)} fusion(f32[2048,64]{1,0:T(8,128)S(1)} %all_gather.11, f32[64,2048]{1,0:T(8,128)S(1)} %copy-done), kind=kOutput, calls=%fused_computation.3 | convolution fusion | flops 100663296 | bytes 1064960 | tf_op jit(solution)/shard_map/dot_general | solution.py:27
  137.7 0.7 copy.12
Async XLA Ops:
  0.6 135.2 %copy-start = (f32[64,2048]{1,0:T(8,128)S(1)}, f32[64,2048]{1,0:T(8,128)}, u32[]{:S(2)}) copy-start(f32[64,2048]{1,0:T(8,128)} %param.17) | copy-start | bytes 1572868
  2.2 46.3 %copy-start.1 = (bf16[2,64,2048]{2,1,0:T(8,128)(2,1)S(1)}, bf16[2,64,2048]{2,1,0:T(8,128)(2,1)}, u32[]{:S(2)}) copy-start(bf16[2,64,2048]{2,1,0:T(8,128)(2,1)} %param.10) | copy-start | bytes 1572868
  48.5 1.1 copy-start.2
  49.5 1.2 copy-start.4
  92.1 1.1 copy-start.5
  92.1 1.1 copy-start.6
  92.1 1.2 copy-start.3
where the time goes:
time: 139 us; the launch traced here: 138 us
  blocking collectives  127 us (91%)
  matrix products  8.74 us (6%)
  other arithmetic  1.5 us (1%)
    all_gather x1, blocking collectives, shards(): right_piece = lax.all_gather(pivot_wide, 'blk', axis=0, tiled=True)  46.3 us
    all_gather x1, blocking collectives, shards(): lax.all_gather(pivot_new, 'blk', axis=0, tiled=True)  40.9 us
    all_gather x1, blocking collectives, shards(): solved_piece = lax.all_gather(finished, 'blk', axis=0, tiled=True)  39.5 us

commit v1 on v0

v1 whole, which is shorter than its diff:
```python
import jax
import jax.numpy as jnp
from jax import lax
from jax.sharding import PartitionSpec as P

HIGH = lax.Precision.HIGHEST
AXIS = "blk"


def stages_of(count):
    bits = count.bit_length() - 1
    fields = []
    top = bits
    while top > 1:
        width = min(2, top - 1)
        top -= width
        fields.append((top, width))
    if bits:
        fields.append((0, 1))
    return fields


def exchange(block, low, width, count):
    mine = (lax.axis_index(AXIS) >> low) & ((1 << width) - 1)
    parts = [block]
    for step in range(1, 1 << width):
        pairs = [(i, i ^ (step << low)) for i in range(count)]
        parts.append(lax.ppermute(block, AXIS, pairs))
    out = jnp.zeros((1 << width,) + block.shape, block.dtype)
    for step, part in enumerate(parts):
        out = lax.dynamic_update_index_in_dim(out, part, mine ^ step, 0)
    return out


def gather_rows(block, count):
    if count & (count - 1):
        return lax.all_gather(block, AXIS, axis=0, tiled=True)
    fields = stages_of(count)
    out = block
    for low, width in fields:
        out = exchange(out, low, width, count)
    lows = [low for low, _ in fields][::-1]
    order = sorted(range(len(lows)), key=lambda axis: -lows[axis])
    depth = len(lows)
    return out.transpose(tuple(order) + (depth, depth + 1)).reshape(-1, block.shape[-1])


def shards(
    count, panel_left, panel_right, ranks, rhs, pivot_left, pivot_right, finished, pivot_rhs, diag_inverse
):
    kmax = panel_left.shape[1]
    cols = pivot_right.shape[1]
    nrhs = finished.shape[1]
    mask = (jnp.arange(kmax, dtype=jnp.int32)[None, :] < ranks[:, None]).astype(jnp.bfloat16)
    left_m = panel_left * mask[:, :, None]
    right_wide = (panel_right * mask[:, :, None]).astype(jnp.float32)
    mine = jnp.concatenate(
        [pivot_right.astype(jnp.float32), finished, pivot_left.astype(jnp.float32), pivot_rhs], axis=1
    )
    whole = gather_rows(mine, count)
    right_piece = whole[:, :cols]
    solved_piece = whole[:, cols : cols + nrhs]
    left_piece = whole[:, cols + nrhs : 2 * cols + nrhs]
    rhs_piece = whole[:, 2 * cols + nrhs :]
    both = jnp.einsum("rkn,nj->rkj", right_wide, whole[:, : cols + nrhs], precision=HIGH)
    gram_sum = both[:, :, :cols]
    proj_sum = both[:, :, cols:]
    pivot_sum = jnp.dot(right_piece.T, solved_piece, precision=HIGH)
    new_left = jnp.einsum(
        "rkj,rkn->rjn", gram_sum.astype(jnp.bfloat16), left_m, preferred_element_type=jnp.float32
    ).astype(jnp.bfloat16)
    new_rhs = rhs - jnp.einsum("rkj,rkn->rjn", proj_sum, left_m.astype(jnp.float32), precision=HIGH)
    pivot_new = rhs_piece - jnp.dot(left_piece, pivot_sum, precision=HIGH)
    next_solution = jnp.dot(diag_inverse, pivot_new, precision=HIGH)
    return (new_left, new_rhs, next_solution)


def solution(mesh):
    count = mesh.shape[AXIS]
    tile = P(AXIS, None, None)
    row = P(AXIS, None)
    in_specs = (tile, tile, P(AXIS), tile, row, row, row, row, row)

    def local(*args):
        return shards(count, *args)

    return jax.shard_map(local, mesh=mesh, in_specs=in_specs, out_specs=(tile, tile, row), check_vma=False)
```

time: 139 us -> 45 us (0.32)
  blocking collectives: 127 us -> 0 us
  waiting for transfers between devices: 0 us -> 14.7 us
  starting transfers between devices: 0 us -> 9.26 us
  local copies, waits for them, and re-layouts: 0.74 us -> 7.6 us
    all_gather x3 -> x0, blocking collectives: 127 us -> none  [the longest x1 46.3 us: shards(): right_piece = lax.all_gather(pivot_wide, 'blk', axis=0, tiled=True)]
    ppermute x0 -> x7, waiting for transfers between devices: none -> 14.7 us  [exchange(): parts.append(lax.ppermute(block, AXIS, pairs))]
    ppermute x0 -> x7, starting transfers between devices: none -> 9.26 us  [exchange(): parts.append(lax.ppermute(block, AXIS, pairs))]
    dynamic_update_slice x0 -> x9, local copies, waits for them, and re-layouts: none -> 5.56 us  [exchange(): out = lax.dynamic_update_index_in_dim(out, part, mine ^ step, 0)]
    dot_general x4 -> x3, matrix products: 4.08 us -> 4.91 us  [the longest x1 2.12 us: shards(): next_solution = jnp.dot(diag_inverse, pivot_new, precision=HIGH)]
  transfers between devices with their start and end apart: 0 -> 7, of which waited for: 0 -> 5; matrix products, arithmetic and copies ran while one was open for 0% -> 11% of each run, Pallas kernels for 0% -> 0%
where the time goes in v1:
time: 45 us; the launch traced here: 44.6 us
  waiting for transfers between devices  14.7 us (33%)
  matrix products  9.89 us (22%)
  starting transfers between devices  9.26 us (21%)
  local copies, waits for them, and re-layouts  7.6 us (17%)
  other arithmetic  2.46 us (5%)
  between operations  0.76 us (2%)
    ppermute x7, waiting for transfers between devices, exchange(): parts.append(lax.ppermute(block, AXIS, pairs))  14.7 us
    ppermute x7, starting transfers between devices, exchange(): parts.append(lax.ppermute(block, AXIS, pairs))  9.26 us
    dynamic_update_slice x9, local copies, waits for them, and re-layouts, exchange(): out = lax.dynamic_update_index_in_dim(out, part, mine ^ step, 0)  5.56 us
    dot_general x1, matrix products, shards(): pivot_sum = jnp.dot(right_piece.T, solved_piece, precision=HIGH)  2.16 us
    dot_general x1, matrix products, shards(): next_solution = jnp.dot(diag_inverse, pivot_new, precision=HIGH)  2.12 us
    dot_general x1, matrix products, shards(): jnp.einsum('rkn,nj->rkj', right_wide, whole[:, :cols + nrhs], precision=H...  1.83 us
    dot_general x1, matrix products, shards(): jnp.einsum('rkj,rkn->rjn', proj_sum, left_m.astype(jnp.float32), precisio...  1.65 us
    broadcast_in_dim x3, local copies, waits for them, and re-layouts, exchange(): out = jnp.zeros((1 << width,) + block.shape, block.dtype)  1.32 us
  transfers between devices with their start and end apart: 7, of which 5 were waited for; matrix products, arithmetic and copies ran while one was open for 11% of the time, Pallas kernels for 0%

profile of v1, /device:TPU:0, one launch (start us, length us, event | category | flops | bytes accessed | tf_op | source)
XLA Modules:
  0.0 44.6 jit_solution(2188293040812085631)
XLA Ops:
  0.6 0.0 copy-start
  0.7 0.8 %convert_element_type.20 = f32[64,64]{1,0:T(8,128)S(1)} convert(bf16[64,64]{1,0:T(8,128)(2,1)} %param.14) | non-fusion elementwise | flops 4096 | bytes 24576 | tf_op jit(solution)/shard_map/convert_element_type | solution.py:58
  1.4 0.7 %convert_element_type.21 = f32[64,64]{1,0:T(8,128)S(1)} convert(bf16[64,64]{1,0:T(8,128)(2,1)} %param.13) | non-fusion elementwise | flops 4096 | bytes 24576 | tf_op jit(solution)/shard_map/convert_element_type | solution.py:58
  2.2 0.9 %bitcast_dynamic-update-slice_fusion.9 = (f32[4,64,256]{2,1,0:T(8,128)S(1)}, f32[64,256]{1,0:T(8,128)S(1)}) fusion(f32[4,64,256]{2,1,0:T(8,128)S(1)} %broadcast_in_dim.48, s32[]{:T(128)S(6)} %select_n.33, f32[64,64]{1,0:T(8,128)} %param.16, f32[64,64]{1,0:T(8,128)S(1)} %convert_element_type.21, f32[64,64]{1,0:T(8,128)} %param.15, ...), kind=kLoop, calls=%fused_computation.29 | loop fusion | flops 49152 | bytes 229380 | tf_op jit(solution)/shard_map/jit(dynamic_update_index_in_dim)/dynamic_update_slice | solution.py:31
  3.1 3.1 %collective-permute-start = (f32[64,256]{1,0:T(8,128)S(1)}, f32[64,256]{1,0:T(8,128)S(1)}, u32[]{:S(2)}, u32[]{:S(2)}) collective-permute-start(f32[64,256]{1,0:T(8,128)S(1)} %get-tuple-element.7), channel_id=1, source_target_pairs={{0,8},{1,9},{2,10},{3,11},{4,12},{5,13},{6,14},{7,15},{8,0},{9,1},... | collective-permute-start | bytes 196616 | tf_op jit(solution)/shard_map/ppermute | solution.py:28
  6.2 2.6 %collective-permute-start.1 = (f32[64,256]{1,0:T(8,128)S(1)}, f32[64,256]{1,0:T(8,128)S(1)}, u32[]{:S(2)}, u32[]{:S(2)}) collective-permute-start(f32[64,256]{1,0:T(8,128)S(1)} %get-tuple-element.7), channel_id=1, source_target_pairs={{0,16},{1,17},{2,18},{3,19},{4,20},{5,21},{6,22},{7,23},{8,24},{9,... | collective-permute-start | bytes 196616 | tf_op jit(solution)/shard_map/ppermute | solution.py:28
  8.8 4.7 %collective-permute-done.1 = f32[64,256]{1,0:T(8,128)S(1)} collective-permute-done((f32[64,256]{1,0:T(8,128)S(1)}, f32[64,256]{1,0:T(8,128)S(1)}, u32[]{:S(2)}, u32[]{:S(2)}) %collective-permute-start.1) | collective-permute-done | bytes 65568 | tf_op jit(solution)/shard_map/ppermute | solution.py:28
  13.5 1.4 %collective-permute-done.2 = f32[64,256]{1,0:T(8,128)S(1)} collective-permute-done((f32[64,256]{1,0:T(8,128)S(1)}, f32[64,256]{1,0:T(8,128)S(1)}, u32[]{:S(2)}, u32[]{:S(2)}) %collective-permute-start.2) | collective-permute-done | bytes 65568 | tf_op jit(solution)/shard_map/ppermute | solution.py:28
  14.9 1.6 %collective-permute-start.3 = (f32[4,64,256]{2,1,0:T(8,128)S(1)}, f32[4,64,256]{2,1,0:T(8,128)S(1)}, u32[]{:S(2)}, u32[]{:S(2)}) collective-permute-start(f32[4,64,256]{2,1,0:T(8,128)S(1)} %bitcast_dynamic-update-slice_fusion.6), channel_id=1, source_target_pairs={{0,2},{1,3},{2,0},{3,1},{4,6},{5,7},{6,4},{7,5},{8,10},{9,11},{10,... | collective-permute-start | bytes 786440 | tf_op jit(solution)/shard_map/ppermute | solution.py:28
  16.4 1.5 %collective-permute-start.4 = (f32[4,64,256]{2,1,0:T(8,128)S(1)}, f32[4,64,256]{2,1,0:T(8,128)S(1)}, u32[]{:S(2)}, u32[]{:S(2)}) collective-permute-start(f32[4,64,256]{2,1,0:T(8,128)S(1)} %bitcast_dynamic-update-slice_fusion.6), channel_id=1, source_target_pairs={{0,4},{1,5},{2,6},{3,7},{4,0},{5,1},{6,2},{7,3},{8,12},{9,13},{10,... | collective-permute-start | bytes 786440 | tf_op jit(solution)/shard_map/ppermute | solution.py:28
  17.9 0.5 %collective-permute-start.5 = (f32[4,64,256]{2,1,0:T(8,128)S(1)}, f32[4,64,256]{2,1,0:T(8,128)S(1)}, u32[]{:S(2)}, u32[]{:S(2)}) collective-permute-start(f32[4,64,256]{2,1,0:T(8,128)S(1)} %bitcast_dynamic-update-slice_fusion.6), channel_id=1, source_target_pairs={{0,6},{1,7},{2,4},{3,5},{4,2},{5,3},{6,0},{7,1},{8,14},{9,15},{10,... | collective-permute-start | bytes 786440 | tf_op jit(solution)/shard_map/ppermute | solution.py:28
  18.4 1.1 %broadcast_in_dim.47 = f32[4,4,64,256]{3,2,0,1:T(8,128)} broadcast(f32[]{:T(128)} %constant.36.clone.1), dimensions={} | broadcast | bytes 1048580 | tf_op jit(solution)/shard_map/broadcast_in_dim | solution.py:29
  19.5 0.7 %bitcast_dynamic-update-slice_fusion.4 = f32[4,4,64,256]{3,2,0,1:T(8,128)} fusion(f32[4,4,64,256]{3,2,0,1:T(8,128)} %broadcast_in_dim.47, s32[]{:T(128)S(6)} %select_n.37, f32[4,64,256]{2,1,0:T(8,128)S(1)} %bitcast_dynamic-update-slice_fusion.6), kind=kLoop, calls=%fused_computation.18 | loop fusion | bytes 524292 | tf_op jit(solution)/shard_map/jit(dynamic_update_index_in_dim)/dynamic_update_slice | solution.py:31
  20.2 3.9 %collective-permute-done.3 = f32[4,64,256]{2,1,0:T(8,128)S(1)} collective-permute-done((f32[4,64,256]{2,1,0:T(8,128)S(1)}, f32[4,64,256]{2,1,0:T(8,128)S(1)}, u32[]{:S(2)}, u32[]{:S(2)}) %collective-permute-start.3) | collective-permute-done | bytes 262176 | tf_op jit(solution)/shard_map/ppermute | solution.py:28
  24.1 0.7 %bitcast_dynamic-update-slice_fusion.3 = f32[4,4,64,256]{3,2,0,1:T(8,128)} fusion(f32[4,4,64,256]{3,2,0,1:T(8,128)} %bitcast_dynamic-update-slice_fusion.4, s32[]{:T(128)S(6)} %select_n.38, f32[4,64,256]{2,1,0:T(8,128)S(1)} %collective-permute-done.3), kind=kLoop, calls=%fused_computation.17 | loop fusion | bytes 524292 | tf_op jit(solution)/shard_map/jit(dynamic_update_index_in_dim)/dynamic_update_slice | solution.py:31
  24.8 3.4 %collective-permute-done.4 = f32[4,64,256]{2,1,0:T(8,128)S(1)} collective-permute-done((f32[4,64,256]{2,1,0:T(8,128)S(1)}, f32[4,64,256]{2,1,0:T(8,128)S(1)}, u32[]{:S(2)}, u32[]{:S(2)}) %collective-permute-start.4) | collective-permute-done | bytes 262176 | tf_op jit(solution)/shard_map/ppermute | solution.py:28
  28.2 0.7 %bitcast_dynamic-update-slice_fusion.2 = f32[4,4,64,256]{3,2,0,1:T(8,128)} fusion(f32[4,4,64,256]{3,2,0,1:T(8,128)} %bitcast_dynamic-update-slice_fusion.3, s32[]{:T(128)S(6)} %select_n.39, f32[4,64,256]{2,1,0:T(8,128)S(1)} %collective-permute-done.4), kind=kLoop, calls=%fused_computation.16 | loop fusion | bytes 524292 | tf_op jit(solution)/shard_map/jit(dynamic_update_index_in_dim)/dynamic_update_slice | solution.py:31
  28.9 0.0 collective-permute-done.5
  28.9 0.7 %bitcast_dynamic-update-slice_fusion.5 = f32[4,4,64,256]{3,2,0,1:T(8,128)} fusion(f32[4,4,64,256]{3,2,0,1:T(8,128)} %bitcast_dynamic-update-slice_fusion.2, s32[]{:T(128)S(6)} %select_n.40, f32[4,64,256]{2,1,0:T(8,128)S(1)} %collective-permute-done.5), kind=kLoop, calls=%fused_computation.19 | loop fusion | bytes 524292 | tf_op jit(solution)/shard_map/jit(dynamic_update_index_in_dim)/dynamic_update_slice | solution.py:31
  29.6 0.1 compare_convert_fusion
  29.7 0.2 broadcast_in_dim.46
  30.0 1.3 %bitcast_dynamic-update-slice_fusion = f32[2,4,4,64,256]{4,3,0,1,2:T(8,128)S(1)} fusion(f32[2,4,4,64,256]{4,3,0,1,2:T(8,128)S(1)} %broadcast_in_dim.46, s32[]{:T(128)S(6)} %select_n.41, f32[4,4,64,256]{3,2,0,1:T(8,128)} %bitcast_dynamic-update-slice_fusion.5), kind=kLoop, calls=%fused_computation.11 | loop fusion | bytes 2097156 | tf_op jit(solution)/shard_map/jit(dynamic_update_index_in_dim)/dynamic_update_slice | solution.py:31
  31.3 1.4 %collective-permute-done.6 = f32[4,4,64,256]{3,2,0,1:T(8,128)} collective-permute-done((f32[4,4,64,256]{3,2,0,1:T(8,128)}, f32[4,4,64,256]{3,2,0,1:T(8,128)}, u32[]{:S(2)}, u32[]{:S(2)}) %collective-permute-start.6) | collective-permute-done | bytes 1048608 | tf_op jit(solution)/shard_map/ppermute | solution.py:28
  32.6 1.3 %bitcast_dynamic-update-slice_fusion.1 = f32[2,4,4,64,256]{4,3,0,1,2:T(8,128)S(1)} fusion(f32[2,4,4,64,256]{4,3,0,1,2:T(8,128)S(1)} %bitcast_dynamic-update-slice_fusion, s32[]{:T(128)S(6)} %select_n.42, f32[4,4,64,256]{3,2,0,1:T(8,128)} %collective-permute-done.6), kind=kLoop, calls=%fused_computation.12 | loop fusion | bytes 2097156 | tf_op jit(solution)/shard_map/jit(dynamic_update_index_in_dim)/dynamic_update_slice | solution.py:31
  34.0 2.2 %fusion = f32[64,64]{1,0:T(8,128)S(1)} fusion(f32[2048,256]{1,0:T(8,128)S(1)} %bitcast.38), kind=kOutput, calls=%fused_computation.3 | convolution fusion | flops 100663296 | bytes 2113536 | tf_op jit(solution)/shard_map/dot_general | solution.py:68
  36.1 1.0 %fusion.3 = f32[2048,64]{1,0:T(8,128)S(1)} fusion(f32[64,64]{1,0:T(8,128)S(1)} %fusion, f32[2048,256]{1,0:T(8,128)S(1)} %bitcast.39), kind=kOutput, calls=%fused_computation.6 | convolution fusion | flops 100663296 | bytes 1605632 | tf_op jit(solution)/shard_map/dot_general | solution.py:73
  37.1 0.0 copy-start.1
  37.1 2.1 %convolution_bitcast_fusion = f32[64,64]{0,1:T(8,128)S(1)} fusion(f32[64,2048]{1,0:T(8,128)S(1)} %copy-done, f32[2048,64]{1,0:T(8,128)S(1)} %fusion.3, f32[2048,256]{1,0:T(8,128)S(1)} %bitcast.40), kind=kOutput, calls=%fused_computation.2 | convolution fusion | flops 100794368 | bytes 2637824 | tf_op jit(solution)/shard_map/dot_general | solution.py:74
  39.3 0.7 %copy.18 = f32[64,64]{1,0:T(8,128)} copy(f32[64,64]{0,1:T(8,128)S(1)} %convolution_bitcast_fusion) | data formatting | bytes 32768
  40.0 1.8 %fusion.5 = f32[2,64,128]{2,1,0:T(8,128)S(1)} fusion(f32[2048,256]{1,0:T(8,128)S(1)} %bitcast.41, bf16[2,64,2048]{2,1,0:T(8,128)(2,1)} %param.10, bf16[2,64]{1,0:T(2,128)(2,1)S(1)} %compare_convert_fusion), kind=kOutput, calls=%fused_computation.10 | convolution fusion | flops 402915328 | bytes 1638912 | tf_op jit(solution)/shard_map/rkn,nj->rkj/dot_general | solution.py:65
  41.8 1.2 %convolution_convert_fusion = bf16[2,64,2048]{2,1,0:T(8,128)(2,1)} fusion(bf16[2,64,2048]{2,1,0:T(8,128)(2,1)S(1)} %copy-done.1, bf16[2,64]{1,0:T(2,128)(2,1)S(1)} %compare_convert_fusion, f32[2,64,128]{2,1,0:T(8,128)S(1)} %fusion.5), kind=kOutput, calls=%fused_computation.1 | convolution fusion | flops 34078720 | bytes 1081856 | tf_op jit(solution)/shard_map/rkj,rkn->rjn/dot_general | solution.py:69
  43.0 1.7 %convolution_subtract_fusion = f32[2,64,2048]{2,1,0:T(8,128)} fusion(f32[2,64,2048]{2,1,0:T(8,128)S(1)} %copy-done.2, bf16[2,64,2048]{2,1,0:T(8,128)(2,1)S(1)} %copy-done.1, bf16[2,64]{1,0:T(2,128)(2,1)S(1)} %compare_convert_fusion, f32[2,64,128]{2,1,0:T(8,128)S(1)} %fusion.5), kind=kOutput, calls=%fused_computation | convolution fusion | flops 201850880 | bytes 2687232 | tf_op jit(solution)/shard_map/rkj,rkn->rjn/dot_general | solution.py:72
  (13 shorter events, 0.1 us)
Async XLA Ops:
  0.6 36.5 %copy-start = (f32[64,2048]{1,0:T(8,128)S(1)}, f32[64,2048]{1,0:T(8,128)}, u32[]{:S(2)}) copy-start(f32[64,2048]{1,0:T(8,128)} %param.17) | copy-start | bytes 1572868
  1.4 28.2 %copy-start.3 = (s32[2]{0:T(128)S(1)}, s32[2]{0:T(128)}, u32[]{:S(2)}) copy-start(s32[2]{0:T(128)} %param.11) | copy-start | bytes 28
  3.1 5.7 %collective-permute-start = (f32[64,256]{1,0:T(8,128)S(1)}, f32[64,256]{1,0:T(8,128)S(1)}, u32[]{:S(2)}, u32[]{:S(2)}) collective-permute-start(f32[64,256]{1,0:T(8,128)S(1)} %get-tuple-element.7), channel_id=1, source_target_pairs={{0,8},{1,9},{2,10},{3,11},{4,12},{5,13},{6,14},{7,15},{8,0},{9,1},... | collective-permute-start | bytes 196616 | tf_op jit(solution)/shard_map/ppermute | solution.py:28
  6.2 7.3 %collective-permute-start.1 = (f32[64,256]{1,0:T(8,128)S(1)}, f32[64,256]{1,0:T(8,128)S(1)}, u32[]{:S(2)}, u32[]{:S(2)}) collective-permute-start(f32[64,256]{1,0:T(8,128)S(1)} %get-tuple-element.7), channel_id=1, source_target_pairs={{0,16},{1,17},{2,18},{3,19},{4,20},{5,21},{6,22},{7,23},{8,24},{9,... | collective-permute-start | bytes 196616 | tf_op jit(solution)/shard_map/ppermute | solution.py:28
  8.8 6.1 %collective-permute-start.2 = (f32[64,256]{1,0:T(8,128)S(1)}, f32[64,256]{1,0:T(8,128)S(1)}, u32[]{:S(2)}, u32[]{:S(2)}) collective-permute-start(f32[64,256]{1,0:T(8,128)S(1)} %get-tuple-element.7), channel_id=1, source_target_pairs={{0,24},{1,25},{2,26},{3,27},{4,28},{5,29},{6,30},{7,31},{8,16},{9,... | collective-permute-start | bytes 196616 | tf_op jit(solution)/shard_map/ppermute | solution.py:28
  14.9 9.2 %collective-permute-start.3 = (f32[4,64,256]{2,1,0:T(8,128)S(1)}, f32[4,64,256]{2,1,0:T(8,128)S(1)}, u32[]{:S(2)}, u32[]{:S(2)}) collective-permute-start(f32[4,64,256]{2,1,0:T(8,128)S(1)} %bitcast_dynamic-update-slice_fusion.6), channel_id=1, source_target_pairs={{0,2},{1,3},{2,0},{3,1},{4,6},{5,7},{6,4},{7,5},{8,10},{9,11},{10,... | collective-permute-start | bytes 786440 | tf_op jit(solution)/shard_map/ppermute | solution.py:28
  16.4 11.8 %collective-permute-start.4 = (f32[4,64,256]{2,1,0:T(8,128)S(1)}, f32[4,64,256]{2,1,0:T(8,128)S(1)}, u32[]{:S(2)}, u32[]{:S(2)}) collective-permute-start(f32[4,64,256]{2,1,0:T(8,128)S(1)} %bitcast_dynamic-update-slice_fusion.6), channel_id=1, source_target_pairs={{0,4},{1,5},{2,6},{3,7},{4,0},{5,1},{6,2},{7,3},{8,12},{9,13},{10,... | collective-permute-start | bytes 786440 | tf_op jit(solution)/shard_map/ppermute | solution.py:28
  17.9 11.0 %collective-permute-start.5 = (f32[4,64,256]{2,1,0:T(8,128)S(1)}, f32[4,64,256]{2,1,0:T(8,128)S(1)}, u32[]{:S(2)}, u32[]{:S(2)}) collective-permute-start(f32[4,64,256]{2,1,0:T(8,128)S(1)} %bitcast_dynamic-update-slice_fusion.6), channel_id=1, source_target_pairs={{0,6},{1,7},{2,4},{3,5},{4,2},{5,3},{6,0},{7,1},{8,14},{9,15},{10,... | collective-permute-start | bytes 786440 | tf_op jit(solution)/shard_map/ppermute | solution.py:28
  29.6 3.0 %collective-permute-start.6 = (f32[4,4,64,256]{3,2,0,1:T(8,128)}, f32[4,4,64,256]{3,2,0,1:T(8,128)}, u32[]{:S(2)}, u32[]{:S(2)}) collective-permute-start(f32[4,4,64,256]{3,2,0,1:T(8,128)} %bitcast_dynamic-update-slice_fusion.5), channel_id=1, source_target_pairs={{0,1},{1,0},{2,3},{3,2},{4,5},{5,4},{6,7},{7,6},{8,9},{9,8},{10,11... | collective-permute-start | bytes 3145736 | tf_op jit(solution)/shard_map/ppermute | solution.py:28
  37.1 4.7 %copy-start.1 = (bf16[2,64,2048]{2,1,0:T(8,128)(2,1)S(1)}, bf16[2,64,2048]{2,1,0:T(8,128)(2,1)}, u32[]{:S(2)}) copy-start(bf16[2,64,2048]{2,1,0:T(8,128)(2,1)} %param.9) | copy-start | bytes 1572868
  40.0 3.0 %copy-start.2 = (f32[2,64,2048]{2,1,0:T(8,128)S(1)}, f32[2,64,2048]{2,1,0:T(8,128)}, u32[]{:S(2)}) copy-start(f32[2,64,2048]{2,1,0:T(8,128)} %param.12) | copy-start | bytes 3145732

commit v2 on v1

v2 whole, which is shorter than its diff:
```python
import functools

import jax
import jax.numpy as jnp
from jax import lax
from jax.experimental import pallas as pl
from jax.experimental.pallas import tpu as pltpu
from jax.sharding import PartitionSpec as P

AXIS = "blk"
F32 = jnp.float32
BF16 = jnp.bfloat16


def fields_of(count):
    bits = count.bit_length() - 1
    fields = []
    top = bits
    while top > 1:
        width = min(2, top - 1)
        top -= width
        fields.append((top, width))
    if bits:
        fields.append((0, 1))
    return fields


def swap(block, mask, count):
    return lax.ppermute(block, AXIS, [(i, i ^ mask) for i in range(count)])


def exchange(block, low, width, count):
    mine = (lax.axis_index(AXIS) >> low) & ((1 << width) - 1)
    parts = [block] + [swap(block, step << low, count) for step in range(1, 1 << width)]
    out = jnp.zeros((1 << width,) + block.shape, block.dtype)
    for step, part in enumerate(parts):
        out = lax.dynamic_update_index_in_dim(out, part, mine ^ step, 0)
    return out


def gather_rows(block, count):
    if count & (count - 1):
        return lax.all_gather(block, AXIS, axis=0, tiled=True)
    fields = fields_of(count)
    out = block
    for low, width in fields:
        out = exchange(out, low, width, count)
    lows = [low for low, _ in fields][::-1]
    order = sorted(range(len(lows)), key=lambda axis: -lows[axis])
    depth = len(lows)
    return out.transpose(tuple(order) + (depth, depth + 1)).reshape(-1, block.shape[-1])


def gather_pieces(block, count):
    rows, width = block.shape
    fields = fields_of(count)
    if count & (count - 1) or rows % 16 or len(fields) != 3:
        return [gather_rows(block, count)[None]], [None]
    first, second, last = fields
    own = exchange(block, *first, count)
    pieces, masks = [], []
    for step in range(1 << second[1]):
        mask = step << second[0]
        piece = swap(own, mask, count) if step else own
        pieces += [piece, swap(piece, 1, count)]
        masks += [mask, mask ^ 1]
    return pieces, masks


def pack_kernel(right, done, left, side, out):
    out[...] = jnp.concatenate(
        [right[...].astype(F32), done[...], left[...].astype(F32), side[...]], axis=1
    )


def split(value):
    high = value.astype(BF16)
    return high, (value - high.astype(F32)).astype(BF16)


def dot(a, b):
    return jnp.dot(a, b, preferred_element_type=F32)


def finish_kernel(masks, stride, ranks, *refs):
    count = len(masks)
    pieces = refs[:count]
    right, left, side, inverse = refs[count : count + 4]
    new_left, new_rhs, solution_out = refs[count + 4 : count + 7]
    both, other, left_buf, rhs_buf, sems = refs[count + 7 :]
    tiles, kmax, _ = left.shape
    wide = both.shape[1] // 2
    half = wide // 2
    me = lax.axis_index(AXIS)
    for piece, mask in zip(pieces, masks):
        groups, rows, _ = piece.shape
        for group in range(groups):
            if mask is None:
                at = group * rows
            else:
                at = pl.multiple_of(((me ^ mask) & (stride - 1)) * rows + group * stride * rows, rows)
            block = piece[group]
            high, low = split(block[:, :wide])
            both[pl.ds(at, rows), :wide] = high
            both[pl.ds(at, rows), wide:] = low
            high, low = split(block[:, wide:])
            other[pl.ds(at, rows), :wide] = high
            other[pl.ds(at, rows), wide:] = low
    flat = right[...].reshape(tiles * kmax, right.shape[2])
    sums = dot(flat, both[...])
    copies = []
    for tile in range(tiles):
        mine = sums[tile * kmax : (tile + 1) * kmax]
        row = lax.broadcasted_iota(jnp.int32, mine.shape, 0)
        mine = jnp.where(row < ranks[tile], mine, 0.0)
        proj = mine[:, half:wide] + mine[:, wide + half :]
        high, low = split(proj)
        weights = jnp.concatenate([mine[:, :half].astype(BF16), high, low], axis=1)
        product = lax.dot_general(
            weights, left[tile], (((0,), (0,)), ((), ())), preferred_element_type=F32
        )
        left_buf[tile] = product[:half].astype(BF16)
        rhs_buf[tile] = side[tile] - (product[half:wide] + product[wide:])
        for buf, hbm, at in ((left_buf, new_left, 0), (rhs_buf, new_rhs, 1)):
            copy = pltpu.make_async_copy(buf.at[tile], hbm.at[tile], sems.at[tile, at])
            copy.start()
            copies.append(copy)
    cross = lax.dot_general(
        both[:, :wide], both[...], (((0,), (0,)), ((), ())), preferred_element_type=F32
    )
    pivot = cross[:half, half:wide] + cross[:half, wide + half :]
    high, low = split(inverse[...])
    rows = high.shape[0]
    solved = dot(jnp.concatenate([high, low], axis=0), other[...])
    left_part = solved[:rows, :half] + solved[rows:, :half]
    rhs_part = solved[:rows, half:wide] + solved[:rows, wide + half :] + solved[rows:, half:wide]
    solution_out[...] = rhs_part - jnp.dot(
        left_part, pivot, precision=lax.Precision.HIGHEST, preferred_element_type=F32
    )
    for copy in copies:
        copy.wait()


def shards(
    count, panel_left, panel_right, ranks, rhs, pivot_left, pivot_right, finished, pivot_rhs, diag_inverse
):
    tiles, kmax, places = panel_left.shape
    rows, cols = pivot_right.shape
    nrhs = finished.shape[1]
    width = 2 * (cols + nrhs)
    vmem = pl.BlockSpec(memory_space=pltpu.VMEM)
    block = pl.pallas_call(
        pack_kernel,
        out_shape=jax.ShapeDtypeStruct((rows, width), F32),
        in_specs=[vmem] * 4,
        out_specs=vmem,
        name="pack",
    )(pivot_right, finished, pivot_left, pivot_rhs)
    pieces, masks = gather_pieces(block, count)
    stride = 1 << fields_of(count)[0][0]
    return pl.pallas_call(
        functools.partial(finish_kernel, masks, stride),
        out_shape=(
            jax.ShapeDtypeStruct(panel_left.shape, BF16),
            jax.ShapeDtypeStruct(rhs.shape, F32),
            jax.ShapeDtypeStruct((rows, nrhs), F32),
        ),
        in_specs=[pl.BlockSpec(memory_space=pltpu.SMEM)] + [vmem] * (len(pieces) + 4),
        out_specs=(pl.BlockSpec(memory_space=pl.ANY), pl.BlockSpec(memory_space=pl.ANY), vmem),
        scratch_shapes=[
            pltpu.VMEM((places, width), BF16),
            pltpu.VMEM((places, width), BF16),
            pltpu.VMEM(panel_left.shape, BF16),
            pltpu.VMEM(rhs.shape, F32),
            pltpu.SemaphoreType.DMA((tiles, 2)),
        ],
        compiler_params=pltpu.CompilerParams(vmem_limit_bytes=24 * 1024 * 1024),
        name="finish",
    )(ranks, *pieces, panel_right, panel_left, rhs, diag_inverse)


def solution(mesh):
    count = mesh.shape[AXIS]
    tile = P(AXIS, None, None)
    row = P(AXIS, None)
    in_specs = (tile, tile, P(AXIS), tile, row, row, row, row, row)

    def local(*args):
        return shards(count, *args)

    return jax.shard_map(local, mesh=mesh, in_specs=in_specs, out_specs=(tile, tile, row), check_vma=False)
```

time: 45 us -> 37.1 us (0.82)
  matrix products: 9.89 us -> 0 us
  Pallas kernels: 0 us -> 5.48 us
  local copies, waits for them, and re-layouts: 7.6 us -> 4.22 us
  other arithmetic: 2.46 us -> 0 us
  waiting for transfers between devices: 14.7 us -> 16.8 us
    dot_general x6 -> x0, matrix products: 9.89 us -> none  [the longest x1 2.16 us: shards(): pivot_sum = jnp.dot(right_piece.T, solved_piece, precision=HIGH)]
    pallas_call x0 -> x2, Pallas kernels: none -> 5.48 us  [the longest x1 3.91 us: shards(): pl.pallas_call(functools.partial(finish_kernel, masks, stride), out_shape...]
    dynamic_update_slice x9 -> x4, local copies, waits for them, and re-layouts: 5.56 us -> 0.88 us  [exchange(): out = lax.dynamic_update_index_in_dim(out, part, mine ^ step, 0)]
    unnamed x9 -> x10, local copies, waits for them, and re-layouts: 0.72 us -> 3.32 us
    ppermute x7 -> x10, waiting for transfers between devices: 14.7 us -> 16.8 us  [swap(): return lax.ppermute(block, AXIS, [(i, i ^ mask) for i in range(count)])]
    convert_element_type x3 -> x0, other arithmetic: 1.58 us -> none  [the longest x1 0.78 us: shards(): pivot_right.astype(jnp.float32)]
    broadcast_in_dim x3 -> x1, local copies, waits for them, and re-layouts: 1.32 us -> 0.02 us  [exchange(): out = jnp.zeros((1 << width,) + block.shape, block.dtype)]
    dynamic_update_slice x1 -> x0, other arithmetic: 0.87 us -> none  [exchange(): out = lax.dynamic_update_index_in_dim(out, part, mine ^ step, 0)]
  transfers between devices with their start and end apart: 7 -> 10, of which waited for: 5 -> 7; matrix products, arithmetic and copies ran while one was open for 11% -> 2% of each run, Pallas kernels for 0% -> 0%
where the time goes in v2:
time: 37.1 us; the launch traced here: 36.8 us
  waiting for transfers between devices  16.8 us (45%)
  starting transfers between devices  9.52 us (26%)
  Pallas kernels  5.48 us (15%)
  local copies, waits for them, and re-layouts  4.22 us (11%)
  between operations  0.69 us (2%)
    ppermute x10, waiting for transfers between devices, swap(): return lax.ppermute(block, AXIS, [(i, i ^ mask) for i in range(count)])  16.8 us
    ppermute x10, starting transfers between devices, swap(): return lax.ppermute(block, AXIS, [(i, i ^ mask) for i in range(count)])  9.52 us
    pallas_call x1, Pallas kernels, shards(): pl.pallas_call(functools.partial(finish_kernel, masks, stride), out_shape...  3.91 us
    unnamed x10, local copies, waits for them, and re-layouts  3.32 us
    pallas_call x1, Pallas kernels, shards(): pl.pallas_call(pack_kernel, out_shape=jax.ShapeDtypeStruct((rows, width),...  1.58 us
    dynamic_update_slice x4, local copies, waits for them, and re-layouts, exchange(): out = lax.dynamic_update_index_in_dim(out, part, mine ^ step, 0)  0.88 us
  transfers between devices with their start and end apart: 10, of which 7 were waited for; matrix products, arithmetic and copies ran while one was open for 2% of the time, Pallas kernels for 0%

profile of v2, /device:TPU:0, one launch (start us, length us, event | category | flops | bytes accessed | tf_op | source)
XLA Modules:
  0.0 36.8 jit_solution(1796526232658482727)
XLA Ops:
  0.6 0.0 copy-start.1
  0.6 1.6 %pack.1 = f32[64,256]{1,0:T(8,128)} custom-call(bf16[64,64]{1,0:T(8,128)(2,1)} %right.1, f32[64,64]{1,0:T(8,128)} %done.1, bf16[64,64]{1,0:T(8,128)(2,1)} %left.1, f32[64,64]{1,0:T(8,128)} %side.1), custom_call_target="tpu_custom_call" | custom-call | tf_op jit(solution)/shard_map/pack/pallas_call | solution.py:152
  2.2 5.1 %collective-permute-start.2 = (f32[64,256]{1,0:T(8,128)}, f32[64,256]{1,0:T(8,128)S(1)}, u32[]{:S(2)}, u32[]{:S(2)}) collective-permute-start(f32[64,256]{1,0:T(8,128)} %pack.1), channel_id=1, source_target_pairs={{0,24},{1,25},{2,26},{3,27},{4,28},{5,29},{6,30},{7,31},{8,16},{9,... | collective-permute-start | bytes 196616 | tf_op jit(solution)/shard_map/ppermute | solution.py:29
  7.3 0.0 collective-permute-start.1
  7.3 0.6 %collective-permute-start = (f32[64,256]{1,0:T(8,128)}, f32[64,256]{1,0:T(8,128)S(1)}, u32[]{:S(2)}, u32[]{:S(2)}) collective-permute-start(f32[64,256]{1,0:T(8,128)} %pack.1), channel_id=1, source_target_pairs={{0,8},{1,9},{2,10},{3,11},{4,12},{5,13},{6,14},{7,15},{8,0},{9,1},... | collective-permute-start | bytes 196616 | tf_op jit(solution)/shard_map/ppermute | solution.py:29
  7.9 0.9 %bitcast_dynamic-update-slice_fusion.3 = f32[4,64,256]{2,1,0:T(8,128)S(1)} fusion(f32[4,64,256]{2,1,0:T(8,128)S(1)} %broadcast_in_dim.16, s32[]{:T(128)S(6)} %select_n.13, f32[64,256]{1,0:T(8,128)} %pack.1), kind=kLoop, calls=%fused_computation.3 | loop fusion | bytes 131076 | tf_op jit(solution)/shard_map/jit(dynamic_update_index_in_dim)/dynamic_update_slice | solution.py:37
  8.7 3.1 %collective-permute-done = f32[64,256]{1,0:T(8,128)S(1)} collective-permute-done((f32[64,256]{1,0:T(8,128)}, f32[64,256]{1,0:T(8,128)S(1)}, u32[]{:S(2)}, u32[]{:S(2)}) %collective-permute-start) | collective-permute-done | bytes 65568 | tf_op jit(solution)/shard_map/ppermute | solution.py:29
  11.8 1.3 %collective-permute-done.1 = f32[64,256]{1,0:T(8,128)S(1)} collective-permute-done((f32[64,256]{1,0:T(8,128)}, f32[64,256]{1,0:T(8,128)S(1)}, u32[]{:S(2)}, u32[]{:S(2)}) %collective-permute-start.1) | collective-permute-done | bytes 65568 | tf_op jit(solution)/shard_map/ppermute | solution.py:29
  13.1 0.0 copy-start.4
  13.1 0.0 collective-permute-done.2
  13.2 2.5 %collective-permute-start.8 = (f32[4,64,256]{2,1,0:T(8,128)S(1)}, f32[4,64,256]{2,1,0:T(8,128)S(1)}, u32[]{:S(2)}, u32[]{:S(2)}) collective-permute-start(f32[4,64,256]{2,1,0:T(8,128)S(1)} %bitcast_dynamic-update-slice_fusion.refs_0_), channel_id=1, source_target_pairs={{0,6},{1,7},{2,4},{3,5},{4,2},{5,3},{6,0},{7,1},{8,14},{9,15},{10,... | collective-permute-start | bytes 786440 | tf_op jit(solution)/shard_map/ppermute | solution.py:29
  15.7 0.5 %collective-permute-start.6 = (f32[4,64,256]{2,1,0:T(8,128)S(1)}, f32[4,64,256]{2,1,0:T(8,128)S(1)}, u32[]{:S(2)}, u32[]{:S(2)}) collective-permute-start(f32[4,64,256]{2,1,0:T(8,128)S(1)} %bitcast_dynamic-update-slice_fusion.refs_0_), channel_id=1, source_target_pairs={{0,4},{1,5},{2,6},{3,7},{4,0},{5,1},{6,2},{7,3},{8,12},{9,13},{10,... | collective-permute-start | bytes 786440 | tf_op jit(solution)/shard_map/ppermute | solution.py:29
  16.2 0.5 %collective-permute-start.4 = (f32[4,64,256]{2,1,0:T(8,128)S(1)}, f32[4,64,256]{2,1,0:T(8,128)S(1)}, u32[]{:S(2)}, u32[]{:S(2)}) collective-permute-start(f32[4,64,256]{2,1,0:T(8,128)S(1)} %bitcast_dynamic-update-slice_fusion.refs_0_), channel_id=1, source_target_pairs={{0,2},{1,3},{2,0},{3,1},{4,6},{5,7},{6,4},{7,5},{8,10},{9,11},{10,... | collective-permute-start | bytes 786440 | tf_op jit(solution)/shard_map/ppermute | solution.py:29
  16.7 0.0 collective-permute-start.3
  16.7 6.6 %collective-permute-done.8.refs_6_ = f32[4,64,256]{2,1,0:T(8,128)S(1)} collective-permute-done((f32[4,64,256]{2,1,0:T(8,128)S(1)}, f32[4,64,256]{2,1,0:T(8,128)S(1)}, u32[]{:S(2)}, u32[]{:S(2)}) %collective-permute-start.8) | collective-permute-done | bytes 262176 | tf_op jit(solution)/shard_map/ppermute | solution.py:29
  23.3 0.0 collective-permute-start.9
  23.4 4.3 %collective-permute-done.6.refs_4_ = f32[4,64,256]{2,1,0:T(8,128)S(1)} collective-permute-done((f32[4,64,256]{2,1,0:T(8,128)S(1)}, f32[4,64,256]{2,1,0:T(8,128)S(1)}, u32[]{:S(2)}, u32[]{:S(2)}) %collective-permute-start.6) | collective-permute-done | bytes 262176 | tf_op jit(solution)/shard_map/ppermute | solution.py:29
  27.6 0.0 collective-permute-start.7
  27.6 0.2 collective-permute-done.4.refs_2_
  27.8 0.3 collective-permute-start.5
  28.1 0.0 collective-permute-done.3.refs_1_
  28.1 0.0 collective-permute-done.9.refs_7_
  28.1 1.0 %collective-permute-done.7.refs_5_ = f32[4,64,256]{2,1,0:T(8,128)S(1)} collective-permute-done((f32[4,64,256]{2,1,0:T(8,128)S(1)}, f32[4,64,256]{2,1,0:T(8,128)S(1)}, u32[]{:S(2)}, u32[]{:S(2)}) %collective-permute-start.7) | collective-permute-done | bytes 262176 | tf_op jit(solution)/shard_map/ppermute | solution.py:29
  29.2 0.4 %collective-permute-done.5.refs_3_ = f32[4,64,256]{2,1,0:T(8,128)S(1)} collective-permute-done((f32[4,64,256]{2,1,0:T(8,128)S(1)}, f32[4,64,256]{2,1,0:T(8,128)S(1)}, u32[]{:S(2)}, u32[]{:S(2)}) %collective-permute-start.5) | collective-permute-done | bytes 262176 | tf_op jit(solution)/shard_map/ppermute | solution.py:29
  29.5 0.0 copy-done.1
  29.5 0.0 copy-done.4
  29.5 0.0 copy-start
  29.5 1.2 %copy-done = f32[2,64,2048]{2,1,0:T(8,128)S(1)} copy-done((f32[2,64,2048]{2,1,0:T(8,128)S(1)}, f32[2,64,2048]{2,1,0:T(8,128)}, u32[]{:S(2)}) %copy-start) | copy-done | bytes 1048600
  30.8 0.0 copy-start.2
  30.8 1.0 %copy-done.2 = bf16[2,64,2048]{2,1,0:T(8,128)(2,1)S(1)} copy-done((bf16[2,64,2048]{2,1,0:T(8,128)(2,1)S(1)}, bf16[2,64,2048]{2,1,0:T(8,128)(2,1)}, u32[]{:S(2)}) %copy-start.2) | copy-done | bytes 524312
  31.8 1.0 %copy-done.3 = f32[64,2048]{1,0:T(8,128)S(1)} copy-done((f32[64,2048]{1,0:T(8,128)S(1)}, f32[64,2048]{1,0:T(8,128)}, u32[]{:S(2)}) %copy-start.3) | copy-done | bytes 524312
  32.8 3.9 %finish.1 = (bf16[2,64,2048]{2,1,0:T(8,128)(2,1)}, f32[2,64,2048]{2,1,0:T(8,128)}, f32[64,64]{1,0:T(8,128)}) custom-call(s32[2]{0:T(128)S(1)} %copy-done.4, f32[4,64,256]{2,1,0:T(8,128)S(1)} %bitcast_dynamic-update-slice_fusion.refs_0_, f32[4,64,256]{2,1,0:T(8,128)S(1)} %collective-permute-done.3.refs_1_, f32[4,64,256]{2,1,0:T(8,128)S(1)} %collective-permute-done.4.refs_2_, ...), custom_call_target="tpu_custom_call" | custom-call | tf_op jit(solution)/shard_map/finish/pallas_call | solution.py:161
  (5 shorter events, 0.0 us)
Async XLA Ops:
  0.6 28.9 %copy-start.1 = (bf16[2,64,2048]{2,1,0:T(8,128)(2,1)S(1)}, bf16[2,64,2048]{2,1,0:T(8,128)(2,1)}, u32[]{:S(2)}) copy-start(bf16[2,64,2048]{2,1,0:T(8,128)(2,1)} %refs_8_.1) | copy-start | bytes 1572868
  2.2 10.9 %collective-permute-start.2 = (f32[64,256]{1,0:T(8,128)}, f32[64,256]{1,0:T(8,128)S(1)}, u32[]{:S(2)}, u32[]{:S(2)}) collective-permute-start(f32[64,256]{1,0:T(8,128)} %pack.1), channel_id=1, source_target_pairs={{0,24},{1,25},{2,26},{3,27},{4,28},{5,29},{6,30},{7,31},{8,16},{9,... | collective-permute-start | bytes 196616 | tf_op jit(solution)/shard_map/ppermute | solution.py:29
  7.3 5.8 %collective-permute-start.1 = (f32[64,256]{1,0:T(8,128)}, f32[64,256]{1,0:T(8,128)S(1)}, u32[]{:S(2)}, u32[]{:S(2)}) collective-permute-start(f32[64,256]{1,0:T(8,128)} %pack.1), channel_id=1, source_target_pairs={{0,16},{1,17},{2,18},{3,19},{4,20},{5,21},{6,22},{7,23},{8,24},{9,... | collective-permute-start | bytes 196616 | tf_op jit(solution)/shard_map/ppermute | solution.py:29
  7.3 4.5 %collective-permute-start = (f32[64,256]{1,0:T(8,128)}, f32[64,256]{1,0:T(8,128)S(1)}, u32[]{:S(2)}, u32[]{:S(2)}) collective-permute-start(f32[64,256]{1,0:T(8,128)} %pack.1), channel_id=1, source_target_pairs={{0,8},{1,9},{2,10},{3,11},{4,12},{5,13},{6,14},{7,15},{8,0},{9,1},... | collective-permute-start | bytes 196616 | tf_op jit(solution)/shard_map/ppermute | solution.py:29
  13.1 16.4 %copy-start.4 = (s32[2]{0:T(128)S(1)}, s32[2]{0:T(128)}, u32[]{:S(2)}) copy-start(s32[2]{0:T(128)} %ranks.1) | copy-start | bytes 28
  13.2 10.2 %collective-permute-start.8 = (f32[4,64,256]{2,1,0:T(8,128)S(1)}, f32[4,64,256]{2,1,0:T(8,128)S(1)}, u32[]{:S(2)}, u32[]{:S(2)}) collective-permute-start(f32[4,64,256]{2,1,0:T(8,128)S(1)} %bitcast_dynamic-update-slice_fusion.refs_0_), channel_id=1, source_target_pairs={{0,6},{1,7},{2,4},{3,5},{4,2},{5,3},{6,0},{7,1},{8,14},{9,15},{10,... | collective-permute-start | bytes 786440 | tf_op jit(solution)/shard_map/ppermute | solution.py:29
  15.7 11.9 %collective-permute-start.6 = (f32[4,64,256]{2,1,0:T(8,128)S(1)}, f32[4,64,256]{2,1,0:T(8,128)S(1)}, u32[]{:S(2)}, u32[]{:S(2)}) collective-permute-start(f32[4,64,256]{2,1,0:T(8,128)S(1)} %bitcast_dynamic-update-slice_fusion.refs_0_), channel_id=1, source_target_pairs={{0,4},{1,5},{2,6},{3,7},{4,0},{5,1},{6,2},{7,3},{8,12},{9,13},{10,... | collective-permute-start | bytes 786440 | tf_op jit(solution)/shard_map/ppermute | solution.py:29
  16.2 11.7 %collective-permute-start.4 = (f32[4,64,256]{2,1,0:T(8,128)S(1)}, f32[4,64,256]{2,1,0:T(8,128)S(1)}, u32[]{:S(2)}, u32[]{:S(2)}) collective-permute-start(f32[4,64,256]{2,1,0:T(8,128)S(1)} %bitcast_dynamic-update-slice_fusion.refs_0_), channel_id=1, source_target_pairs={{0,2},{1,3},{2,0},{3,1},{4,6},{5,7},{6,4},{7,5},{8,10},{9,11},{10,... | collective-permute-start | bytes 786440 | tf_op jit(solution)/shard_map/ppermute | solution.py:29
  16.7 11.4 %collective-permute-start.3 = (f32[4,64,256]{2,1,0:T(8,128)S(1)}, f32[4,64,256]{2,1,0:T(8,128)S(1)}, u32[]{:S(2)}, u32[]{:S(2)}) collective-permute-start(f32[4,64,256]{2,1,0:T(8,128)S(1)} %bitcast_dynamic-update-slice_fusion.refs_0_), channel_id=1, source_target_pairs={{0,1},{1,0},{2,3},{3,2},{4,5},{5,4},{6,7},{7,6},{8,9},{9,8},{10,11... | collective-permute-start | bytes 786440 | tf_op jit(solution)/shard_map/ppermute | solution.py:29
  23.3 4.8 %collective-permute-start.9 = (f32[4,64,256]{2,1,0:T(8,128)S(1)}, f32[4,64,256]{2,1,0:T(8,128)S(1)}, u32[]{:S(2)}, u32[]{:S(2)}) collective-permute-start(f32[4,64,256]{2,1,0:T(8,128)S(1)} %collective-permute-done.8.refs_6_), channel_id=1, source_target_pairs={{0,1},{1,0},{2,3},{3,2},{4,5},{5,4},{6,7},{7,6},{8,9},{9,8},{10,11... | collective-permute-start | bytes 786440 | tf_op jit(solution)/shard_map/ppermute | solution.py:29
  27.6 1.5 %collective-permute-start.7 = (f32[4,64,256]{2,1,0:T(8,128)S(1)}, f32[4,64,256]{2,1,0:T(8,128)S(1)}, u32[]{:S(2)}, u32[]{:S(2)}) collective-permute-start(f32[4,64,256]{2,1,0:T(8,128)S(1)} %collective-permute-done.6.refs_4_), channel_id=1, source_target_pairs={{0,1},{1,0},{2,3},{3,2},{4,5},{5,4},{6,7},{7,6},{8,9},{9,8},{10,11... | collective-permute-start | bytes 786440 | tf_op jit(solution)/shard_map/ppermute | solution.py:29
  27.8 1.7 %collective-permute-start.5 = (f32[4,64,256]{2,1,0:T(8,128)S(1)}, f32[4,64,256]{2,1,0:T(8,128)S(1)}, u32[]{:S(2)}, u32[]{:S(2)}) collective-permute-start(f32[4,64,256]{2,1,0:T(8,128)S(1)} %collective-permute-done.4.refs_2_), channel_id=1, source_target_pairs={{0,1},{1,0},{2,3},{3,2},{4,5},{5,4},{6,7},{7,6},{8,9},{9,8},{10,11... | collective-permute-start | bytes 786440 | tf_op jit(solution)/shard_map/ppermute | solution.py:29
  29.5 1.2 %copy-start = (f32[2,64,2048]{2,1,0:T(8,128)S(1)}, f32[2,64,2048]{2,1,0:T(8,128)}, u32[]{:S(2)}) copy-start(f32[2,64,2048]{2,1,0:T(8,128)} %refs_10_.1) | copy-start | bytes 3145732
  30.8 1.0 %copy-start.2 = (bf16[2,64,2048]{2,1,0:T(8,128)(2,1)S(1)}, bf16[2,64,2048]{2,1,0:T(8,128)(2,1)}, u32[]{:S(2)}) copy-start(bf16[2,64,2048]{2,1,0:T(8,128)(2,1)} %refs_9_.1) | copy-start | bytes 1572868
  31.8 1.0 %copy-start.3 = (f32[64,2048]{1,0:T(8,128)S(1)}, f32[64,2048]{1,0:T(8,128)}, u32[]{:S(2)}) copy-start(f32[64,2048]{1,0:T(8,128)} %refs_11_.1) | copy-start | bytes 1572868

commit v3 on v1

v3 whole, which is shorter than its diff:
```python
import functools

import jax
import jax.numpy as jnp
from jax import lax
from jax.experimental import pallas as pl
from jax.experimental.pallas import tpu as pltpu
from jax.sharding import PartitionSpec as P


AXIS = "blk"
PARTS = 2
F32 = jnp.float32
BF16 = jnp.bfloat16
VMEM = pl.BlockSpec(memory_space=pltpu.VMEM)
HBM = pl.BlockSpec(memory_space=pltpu.HBM)


def fields_of(count):
    bits = count.bit_length() - 1
    fields = []
    top = bits
    while top > 1:
        width = min(2, top - 1)
        top -= width
        fields.append((top, width))
    if bits:
        fields.append((0, 1))
    return fields


def swap(block, mask, count):
    return lax.ppermute(block, AXIS, [(i, i ^ mask) for i in range(count)])


def exchange(block, low, width, count):
    mine = (lax.axis_index(AXIS) >> low) & ((1 << width) - 1)
    parts = [block] + [swap(block, step << low, count) for step in range(1, 1 << width)]
    out = jnp.zeros((1 << width,) + block.shape, block.dtype)
    for step, part in enumerate(parts):
        out = lax.dynamic_update_index_in_dim(out, part, mine ^ step, 0)
    return out


def gather_rows(block, count):
    if count & (count - 1):
        return lax.all_gather(block, AXIS, axis=0, tiled=True)
    fields = fields_of(count)
    out = block
    for low, width in fields:
        out = exchange(out, low, width, count)
    lows = [low for low, _ in fields][::-1]
    order = sorted(range(len(lows)), key=lambda axis: -lows[axis])
    depth = len(lows)
    return out.transpose(tuple(order) + (depth, depth + 1)).reshape(-1, block.shape[-1])


def squares(count):
    return not count & (count - 1) and [wide for _, wide in fields_of(count)] == [2, 2, 1]


def gather_halves(block, count):
    _, width = block.shape
    fields = fields_of(count)
    if not squares(count):
        whole = gather_rows(block, count).reshape(2, 1, -1, width)
        return [[(whole[0], None)], [(whole[1], None)]]
    (first, _), (second, _), _ = fields
    steps = [step << first for step in range(4)]
    blocks = [block] + [swap(block, step << first, count) for step in range(1, 4)]
    halves = []
    for at in (0, 2):
        own = jnp.stack(blocks[at : at + 2])
        half = []
        for step in range(4):
            mask = step << second
            piece = swap(own, mask, count) if step else own
            other = swap(piece, 1, count)
            for core, part in ((0, piece), (1, other)):
                half.append((part, [mask ^ core ^ plane for plane in steps[at : at + 2]]))
        halves.append(half)
    return halves


def pack_kernel(right, done, left, side, out, right_buf, done_buf, left_buf, side_buf, sems):
    pairs = ((right, right_buf), (done, done_buf), (left, left_buf), (side, side_buf))
    copies = [pltpu.make_async_copy(hbm, buf, sems.at[at]) for at, (hbm, buf) in enumerate(pairs)]
    for copy in copies:
        copy.start()
    for copy in copies:
        copy.wait()
    out[...] = jnp.concatenate(
        [right_buf[...].astype(F32), done_buf[...], left_buf[...].astype(F32), side_buf[...]], axis=1
    )


def split(value):
    high = value.astype(BF16)
    return high, (value - high.astype(F32)).astype(BF16)


def dot(a, b):
    return jnp.dot(a, b, preferred_element_type=F32)


def dot_rows(a, b):
    return lax.dot_general(a, b, (((0,), (0,)), ((), ())), preferred_element_type=F32)


def start_of(pieces, masks, index, length):
    if masks[0] is None:
        return index * length
    here = (lax.axis_index(AXIS) ^ masks[0][0]) * pieces[0].shape[1]
    return pl.multiple_of(here // length * length, length)


def fill(pieces, masks, buf, offset):
    length, width = buf.shape
    wide = width // 2
    me = lax.axis_index(AXIS)
    for piece, mask in zip(pieces, masks):
        groups, rows, _ = piece.shape
        for group in range(groups):
            at = 0 if mask is None else pl.multiple_of(lax.rem((me ^ mask[group]) * rows, length), rows)
            high, low = split(piece[group, :, offset : offset + wide])
            buf[pl.ds(at, rows), :wide] = high
            buf[pl.ds(at, rows), wide:] = low


def panel_product(pieces, masks, index, right, both):
    length = both.shape[0]
    tiles, kmax, _ = right.shape
    start = start_of(pieces, masks, index, length)
    return dot(right[:, :, pl.ds(start, length)].reshape(tiles * kmax, length), both[...])


def pivot_products(pieces, masks, index, inverse, both, other):
    length, width = both.shape
    start = start_of(pieces, masks, index, length)
    cross = dot_rows(both[:, : width // 4], both[...])
    high, low = split(inverse[:, pl.ds(start, length)])
    return cross, dot(jnp.concatenate([high, low], axis=0), other[...])


def first_kernel(masks, ranks, *refs):
    count = len(masks)
    pieces = refs[:count]
    right, inverse, left, side = refs[count : count + 4]
    sums_out, cross_out, solved_out, keep_out, inverse_out, left_out, side_out = refs[count + 4 : count + 11]
    both, other, sems = refs[count + 11 :]
    pairs = ((inverse, inverse_out), (left, left_out), (side, side_out))
    copies = [pltpu.make_async_copy(hbm, out, sems.at[at]) for at, (hbm, out) in enumerate(pairs)]
    for copy in copies:
        copy.start()
    tiles, kmax, _ = right.shape
    for tile in range(tiles):
        at = pl.ds(tile * kmax, kmax)
        row = lax.broadcasted_iota(jnp.int32, (kmax, keep_out.shape[1]), 0)
        keep_out[at, :] = (row < ranks[tile]).astype(F32)
    fill(pieces, masks, both, 0)
    fill(pieces, masks, other, both.shape[1] // 2)
    sums_out[...] = panel_product(pieces, masks, 0, right, both)
    copies[0].wait()
    cross_out[...], solved_out[...] = pivot_products(pieces, masks, 0, inverse_out, both, other)
    for copy in copies[1:]:
        copy.wait()


def finish_kernel(masks, *refs):
    count = len(masks)
    pieces = refs[:count]
    right, sums_in, cross_in, solved_in, keep, inverse, left, side = refs[count : count + 8]
    new_left, new_rhs, solution_out = refs[count + 8 : count + 11]
    both, other, left_buf, rhs_buf, solution_buf, sems = refs[count + 11 :]
    tiles, kmax, places = left.shape
    wide = both.shape[1] // 2
    half = wide // 2
    fill(pieces, masks, both, 0)
    sums = (panel_product(pieces, masks, 1, right, both) + sums_in[...]) * keep[...]
    fill(pieces, masks, other, wide)
    cross, solved = pivot_products(pieces, masks, 1, inverse, both, other)
    cross += cross_in[...]
    solved += solved_in[...]
    high, low = split(cross[:, half:wide] + cross[:, wide + half :])
    pivot = jnp.concatenate([high, low, high], axis=0)
    rows = solved.shape[0] // 2
    high, low = split(solved[:rows, :half] + solved[rows:, :half])
    rhs_part = solved[:rows, half:wide] + solved[:rows, wide + half :] + solved[rows:, half:wide]
    solution_buf[...] = rhs_part - dot(jnp.concatenate([high, high, low], axis=1), pivot)
    last = pltpu.make_async_copy(solution_buf, solution_out, sems.at[2 * PARTS * tiles])
    last.start()
    copies = []
    span = places // PARTS
    for tile in range(tiles):
        mine = sums[tile * kmax : (tile + 1) * kmax]
        high, low = split(mine[:, half:wide] + mine[:, wide + half :])
        weights = jnp.concatenate([mine[:, :half].astype(BF16), high, low], axis=1)
        for part in range(PARTS):
            at = (tile, slice(None), pl.ds(part * span, span))
            product = dot_rows(weights, left[at])
            left_buf[at] = product[:half].astype(BF16)
            rhs_buf[at] = side[at] - (product[half:wide] + product[wide:])
            for buf, hbm in ((left_buf, new_left), (rhs_buf, new_rhs)):
                copy = pltpu.make_async_copy(buf.at[at], hbm.at[at], sems.at[len(copies)])
                copy.start()
                copies.append(copy)

    for copy in copies + [last]:
        copy.wait()


def shards(
    count, panel_left, panel_right, ranks, rhs, pivot_left, pivot_right, finished, pivot_rhs, diag_inverse
):
    tiles, kmax, places = panel_left.shape
    rows, cols = pivot_right.shape
    nrhs = finished.shape[1]
    width = 2 * (cols + nrhs)
    params = pltpu.CompilerParams(vmem_limit_bytes=20 * 1024 * 1024)
    first_params = pltpu.CompilerParams(vmem_limit_bytes=52_000_000)
    block = pl.pallas_call(
        pack_kernel,
        out_shape=pltpu.VMEM((rows, width), F32),
        in_specs=[HBM] * 4,
        out_specs=VMEM,
        scratch_shapes=[
            pltpu.VMEM((rows, cols), BF16),
            pltpu.VMEM((rows, nrhs), F32),
            pltpu.VMEM((rows, cols), BF16),
            pltpu.VMEM((rows, nrhs), F32),
            pltpu.SemaphoreType.DMA((4,)),
        ],
        name="pack",
    )(pivot_right, finished, pivot_left, pivot_rhs)
    near, far = gather_halves(block, count)
    halves = [pltpu.VMEM((places // 2, width), BF16)] * 2
    middle = pl.pallas_call(
        functools.partial(first_kernel, [mask for _, mask in near]),
        out_shape=(
            pltpu.VMEM((tiles * kmax, width), F32),
            pltpu.VMEM((cols, width), F32),
            pltpu.VMEM((2 * rows, width), F32),
            pltpu.VMEM((tiles * kmax, width), F32),
            pltpu.VMEM(diag_inverse.shape, F32),
            pltpu.VMEM(panel_left.shape, BF16),
            pltpu.VMEM(rhs.shape, F32),
        ),
        in_specs=[pl.BlockSpec(memory_space=pltpu.SMEM)] + [VMEM] * (len(near) + 1) + [HBM] * 3,
        out_specs=(VMEM,) * 7,
        scratch_shapes=halves + [pltpu.SemaphoreType.DMA((3,))],
        compiler_params=first_params,
        cost_estimate=pl.CostEstimate(flops=300_000_000, bytes_accessed=4_000_000, transcendentals=0),
        name="first",
    )(ranks, *[piece for piece, _ in near], panel_right, diag_inverse, panel_left, rhs)
    return pl.pallas_call(
        functools.partial(finish_kernel, [mask for _, mask in far]),
        out_shape=(
            jax.ShapeDtypeStruct(panel_left.shape, BF16),
            jax.ShapeDtypeStruct(rhs.shape, F32),
            jax.ShapeDtypeStruct((rows, nrhs), F32),
        ),
        in_specs=[VMEM] * (len(far) + 8),
        out_specs=(HBM,) * 3,
        scratch_shapes=halves
        + [
            pltpu.VMEM(panel_left.shape, BF16),
            pltpu.VMEM(rhs.shape, F32),
            pltpu.VMEM((rows, nrhs), F32),
            pltpu.SemaphoreType.DMA((2 * PARTS * tiles + 1,)),
        ],
        compiler_params=params,
        name="finish",
    )(*[piece for piece, _ in far], panel_right, *middle)


def solution(mesh):
    count = mesh.shape[AXIS]
    tile = P(AXIS, None, None)
    row = P(AXIS, None)
    in_specs = (tile, tile, P(AXIS), tile, row, row, row, row, row)

    def local(*args):
        return shards(count, *args)

    step = jax.shard_map(local, mesh=mesh, in_specs=in_specs, out_specs=(tile, tile, row), check_vma=False)
    return step if squares(count) else step
```

time: 45 us -> 33.1 us (0.74)
  matrix products: 9.89 us -> 0 us
  local copies, waits for them, and re-layouts: 7.6 us -> 0.01 us
  starting transfers between devices: 9.26 us -> 16.5 us
  Pallas kernels: 0 us -> 5.43 us
  waiting for transfers between devices: 14.7 us -> 10.3 us
  other arithmetic: 2.46 us -> 0.02 us
    dot_general x6 -> x0, matrix products: 9.89 us -> none  [the longest x1 2.16 us: shards(): pivot_sum = jnp.dot(right_piece.T, solved_piece, precision=HIGH)]
    ppermute x7 -> x17, starting transfers between devices: 9.26 us -> 16.5 us  [swap(): return lax.ppermute(block, AXIS, [(i, i ^ mask) for i in range(count)])]
    dynamic_update_slice x9 -> x0, local copies, waits for them, and re-layouts: 5.56 us -> none  [exchange(): out = lax.dynamic_update_index_in_dim(out, part, mine ^ step, 0)]
    pallas_call x0 -> x3, Pallas kernels: none -> 5.43 us  [the longest x1 2.29 us: shards(): pl.pallas_call(functools.partial(first_kernel, [mask for _, mask in near]...]
    ppermute x7 -> x17, waiting for transfers between devices: 14.7 us -> 10.3 us  [swap(): return lax.ppermute(block, AXIS, [(i, i ^ mask) for i in range(count)])]
    convert_element_type x3 -> x0, other arithmetic: 1.58 us -> none  [the longest x1 0.78 us: shards(): pivot_right.astype(jnp.float32)]
    broadcast_in_dim x3 -> x0, local copies, waits for them, and re-layouts: 1.32 us -> none  [exchange(): out = jnp.zeros((1 << width,) + block.shape, block.dtype)]
    dynamic_update_slice x1 -> x0, other arithmetic: 0.87 us -> none  [exchange(): out = lax.dynamic_update_index_in_dim(out, part, mine ^ step, 0)]
  transfers between devices with their start and end apart: 7 -> 17, of which waited for: 5 -> 5; matrix products, arithmetic and copies ran while one was open for 11% -> 0% of each run, Pallas kernels for 0% -> 7%
where the time goes in v3:
time: 33.1 us; the launch traced here: 32.9 us
  starting transfers between devices  16.5 us (50%)
  waiting for transfers between devices  10.3 us (31%)
  Pallas kernels  5.43 us (16%)
  between operations  0.72 us (2%)
    ppermute x17, starting transfers between devices, swap(): return lax.ppermute(block, AXIS, [(i, i ^ mask) for i in range(count)])  16.5 us
    ppermute x17, waiting for transfers between devices, swap(): return lax.ppermute(block, AXIS, [(i, i ^ mask) for i in range(count)])  10.3 us
    pallas_call x1, Pallas kernels, shards(): pl.pallas_call(functools.partial(first_kernel, [mask for _, mask in near]...  2.29 us
    pallas_call x1, Pallas kernels, shards(): pl.pallas_call(functools.partial(finish_kernel, [mask for _, mask in far]...  2.15 us
    pallas_call x1, Pallas kernels, shards(): pl.pallas_call(pack_kernel, out_shape=pltpu.VMEM((rows, width), F32), in_...  0.98 us
  transfers between devices with their start and end apart: 17, of which 5 were waited for; matrix products, arithmetic and copies ran while one was open for 0% of the time, Pallas kernels for 7%

profile of v3, /device:TPU:0, one launch (start us, length us, event | category | flops | bytes accessed | tf_op | source)
XLA Modules:
  0.0 32.9 jit_solution(6234591017368785207)
XLA Ops:
  0.6 1.0 %pack.1 = f32[64,256]{1,0:T(8,128)S(1)} custom-call(bf16[64,64]{1,0:T(8,128)(2,1)} %right.1, f32[64,64]{1,0:T(8,128)} %done.1, bf16[64,64]{1,0:T(8,128)(2,1)} %left.1, f32[64,64]{1,0:T(8,128)} %side.1), custom_call_target="tpu_custom_call" | custom-call | tf_op jit(solution)/shard_map/pack/pallas_call | solution.py:221
  1.6 5.1 %collective-permute-start.1 = (f32[64,256]{1,0:T(8,128)S(1)}, f32[64,256]{1,0:T(8,128)S(1)}, u32[]{:S(2)}, u32[]{:S(2)}) collective-permute-start(f32[64,256]{1,0:T(8,128)S(1)} %pack.1), channel_id=1, source_target_pairs={{0,24},{1,25},{2,26},{3,27},{4,28},{5,29},{6,30},{7,31},{8,16},{9,... | collective-permute-start | bytes 196616 | tf_op jit(solution)/shard_map/ppermute | solution.py:33
  6.8 0.6 %collective-permute-start.9 = (f32[64,256]{1,0:T(8,128)S(1)}, f32[64,256]{1,0:T(8,128)S(1)}, u32[]{:S(2)}, u32[]{:S(2)}) collective-permute-start(f32[64,256]{1,0:T(8,128)S(1)} %pack.1), channel_id=1, source_target_pairs={{0,8},{1,9},{2,10},{3,11},{4,12},{5,13},{6,14},{7,15},{8,0},{9,1},... | collective-permute-start | bytes 196616 | tf_op jit(solution)/shard_map/ppermute | solution.py:33
  7.4 1.8 %collective-permute-done.1 = f32[64,256]{1,0:T(8,128)S(1)} collective-permute-done((f32[64,256]{1,0:T(8,128)S(1)}, f32[64,256]{1,0:T(8,128)S(1)}, u32[]{:S(2)}, u32[]{:S(2)}) %collective-permute-start.1) | collective-permute-done | bytes 65568 | tf_op jit(solution)/shard_map/ppermute | solution.py:33
  9.3 3.1 %collective-permute-done = f32[64,256]{1,0:T(8,128)S(1)} collective-permute-done((f32[64,256]{1,0:T(8,128)S(1)}, f32[64,256]{1,0:T(8,128)S(1)}, u32[]{:S(2)}, u32[]{:S(2)}) %collective-permute-start) | collective-permute-done | bytes 65568 | tf_op jit(solution)/shard_map/ppermute | solution.py:33
  12.4 2.5 %collective-permute-start.7 = (f32[2,64,256]{2,1,0:T(8,128)S(1)}, f32[2,64,256]{2,1,0:T(8,128)S(1)}, u32[]{:S(2)}, u32[]{:S(2)}) collective-permute-start(f32[2,64,256]{2,1,0:T(8,128)S(1)} %pad_maximum_fusion.refs_0_), channel_id=1, source_target_pairs={{0,6},{1,7},{2,4},{3,5},{4,2},{5,3},{6,0},{7,1},{8,14},{9,15},{10,... | collective-permute-start | bytes 393224 | tf_op jit(solution)/shard_map/ppermute | solution.py:33
  14.9 0.5 %collective-permute-start.5 = (f32[2,64,256]{2,1,0:T(8,128)S(1)}, f32[2,64,256]{2,1,0:T(8,128)S(1)}, u32[]{:S(2)}, u32[]{:S(2)}) collective-permute-start(f32[2,64,256]{2,1,0:T(8,128)S(1)} %pad_maximum_fusion.refs_0_), channel_id=1, source_target_pairs={{0,4},{1,5},{2,6},{3,7},{4,0},{5,1},{6,2},{7,3},{8,12},{9,13},{10,... | collective-permute-start | bytes 393224 | tf_op jit(solution)/shard_map/ppermute | solution.py:33
  15.4 0.0 collective-permute-done.9
  15.4 1.6 %collective-permute-start.15 = (f32[2,64,256]{2,1,0:T(8,128)S(1)}, f32[2,64,256]{2,1,0:T(8,128)S(1)}, u32[]{:S(2)}, u32[]{:S(2)}) collective-permute-start(f32[2,64,256]{2,1,0:T(8,128)S(1)} %pad_maximum_fusion.1.refs_0_), channel_id=1, source_target_pairs={{0,6},{1,7},{2,4},{3,5},{4,2},{5,3},{6,0},{7,1},{8,14},{9,15},{10,... | collective-permute-start | bytes 393224 | tf_op jit(solution)/shard_map/ppermute | solution.py:33
  17.0 0.5 %collective-permute-start.13 = (f32[2,64,256]{2,1,0:T(8,128)S(1)}, f32[2,64,256]{2,1,0:T(8,128)S(1)}, u32[]{:S(2)}, u32[]{:S(2)}) collective-permute-start(f32[2,64,256]{2,1,0:T(8,128)S(1)} %pad_maximum_fusion.1.refs_0_), channel_id=1, source_target_pairs={{0,4},{1,5},{2,6},{3,7},{4,0},{5,1},{6,2},{7,3},{8,12},{9,13},{10,... | collective-permute-start | bytes 393224 | tf_op jit(solution)/shard_map/ppermute | solution.py:33
  17.5 1.5 %collective-permute-start.11 = (f32[2,64,256]{2,1,0:T(8,128)S(1)}, f32[2,64,256]{2,1,0:T(8,128)S(1)}, u32[]{:S(2)}, u32[]{:S(2)}) collective-permute-start(f32[2,64,256]{2,1,0:T(8,128)S(1)} %pad_maximum_fusion.1.refs_0_), channel_id=1, source_target_pairs={{0,2},{1,3},{2,0},{3,1},{4,6},{5,7},{6,4},{7,5},{8,10},{9,11},{10,... | collective-permute-start | bytes 393224 | tf_op jit(solution)/shard_map/ppermute | solution.py:33
  19.0 0.0 collective-permute-done.7.refs_6_
  19.0 2.3 %collective-permute-start.3 = (f32[2,64,256]{2,1,0:T(8,128)S(1)}, f32[2,64,256]{2,1,0:T(8,128)S(1)}, u32[]{:S(2)}, u32[]{:S(2)}) collective-permute-start(f32[2,64,256]{2,1,0:T(8,128)S(1)} %pad_maximum_fusion.refs_0_), channel_id=1, source_target_pairs={{0,2},{1,3},{2,0},{3,1},{4,6},{5,7},{6,4},{7,5},{8,10},{9,11},{10,... | collective-permute-start | bytes 393224 | tf_op jit(solution)/shard_map/ppermute | solution.py:33
  21.3 2.8 %collective-permute-done.5.refs_4_ = f32[2,64,256]{2,1,0:T(8,128)S(1)} collective-permute-done((f32[2,64,256]{2,1,0:T(8,128)S(1)}, f32[2,64,256]{2,1,0:T(8,128)S(1)}, u32[]{:S(2)}, u32[]{:S(2)}) %collective-permute-start.5) | collective-permute-done | bytes 131104 | tf_op jit(solution)/shard_map/ppermute | solution.py:33
  24.1 0.5 %collective-permute-start.16 = (f32[2,64,256]{2,1,0:T(8,128)S(1)}, f32[2,64,256]{2,1,0:T(8,128)S(1)}, u32[]{:S(2)}, u32[]{:S(2)}) collective-permute-start(f32[2,64,256]{2,1,0:T(8,128)S(1)} %collective-permute-done.15.refs_6_), channel_id=1, source_target_pairs={{0,1},{1,0},{2,3},{3,2},{4,5},{5,4},{6,7},{7,6},{8,9},{9,8},{10,11... | collective-permute-start | bytes 393224 | tf_op jit(solution)/shard_map/ppermute | solution.py:33
  24.6 2.2 %collective-permute-done.13.refs_4_ = f32[2,64,256]{2,1,0:T(8,128)S(1)} collective-permute-done((f32[2,64,256]{2,1,0:T(8,128)S(1)}, f32[2,64,256]{2,1,0:T(8,128)S(1)}, u32[]{:S(2)}, u32[]{:S(2)}) %collective-permute-start.13) | collective-permute-done | bytes 131104 | tf_op jit(solution)/shard_map/ppermute | solution.py:33
  26.9 0.0 collective-permute-start.14
  26.9 0.0 collective-permute-done.11.refs_2_
  26.9 0.5 %collective-permute-start.12 = (f32[2,64,256]{2,1,0:T(8,128)S(1)}, f32[2,64,256]{2,1,0:T(8,128)S(1)}, u32[]{:S(2)}, u32[]{:S(2)}) collective-permute-start(f32[2,64,256]{2,1,0:T(8,128)S(1)} %collective-permute-done.11.refs_2_), channel_id=1, source_target_pairs={{0,1},{1,0},{2,3},{3,2},{4,5},{5,4},{6,7},{7,6},{8,9},{9,8},{10,11... | collective-permute-start | bytes 393224 | tf_op jit(solution)/shard_map/ppermute | solution.py:33
  27.4 0.0 collective-permute-done.3.refs_2_
  27.4 0.1 collective-permute-start.2
  27.4 0.0 collective-permute-done.10.refs_1_
  27.4 0.4 %collective-permute-start.8 = (f32[2,64,256]{2,1,0:T(8,128)S(1)}, f32[2,64,256]{2,1,0:T(8,128)S(1)}, u32[]{:S(2)}, u32[]{:S(2)}) collective-permute-start(f32[2,64,256]{2,1,0:T(8,128)S(1)} %collective-permute-done.7.refs_6_), channel_id=1, source_target_pairs={{0,1},{1,0},{2,3},{3,2},{4,5},{5,4},{6,7},{7,6},{8,9},{9,8},{10,11... | collective-permute-start | bytes 393224 | tf_op jit(solution)/shard_map/ppermute | solution.py:33
  27.9 0.0 collective-permute-done.16.refs_7_
  27.9 0.1 collective-permute-start.6
  28.0 0.2 collective-permute-done.14.refs_5_
  28.2 0.2 collective-permute-start.4
  28.4 0.0 collective-permute-done.12.refs_3_
  28.4 2.3 %first.1 = (f32[128,256]{1,0:T(8,128)S(1)}, f32[64,256]{1,0:T(8,128)S(1)}, f32[128,256]{1,0:T(8,128)S(1)}, f32[128,256]{1,0:T(8,128)S(1)}, f32[64,2048]{1,0:T(8,...) custom-call(s32[2]{0:T(128)S(1)} %copy-done.1, f32[2,64,256]{2,1,0:T(8,128)S(1)} %pad_maximum_fusion.1.refs_0_, ...), custom_call_target="tpu_custom_call" | custom-call | flops 300000000 | bytes 4000000 | tf_op jit(solution)/shard_map/first/pallas_call | solution.py:237
  30.7 0.0 collective-permute-done.2.refs_1_
  30.7 0.0 collective-permute-done.6.refs_5_
  30.8 2.2 %finish.1 = (bf16[2,64,2048]{2,1,0:T(8,128)(2,1)}, f32[2,64,2048]{2,1,0:T(8,128)}, f32[64,64]{1,0:T(8,128)}) custom-call(f32[2,64,256]{2,1,0:T(8,128)S(1)} %pad_maximum_fusion.refs_0_, f32[2,64,256]{2,1,0:T(8,128)S(1)} %collective-permute-done.2.refs_1_, f32[2,64,256]{2,1,0:T(8,128)S(1)} %collective-permute-done.3.refs_2_, ...), custom_call_target="tpu_custom_call" | custom-call | tf_op jit(solution)/shard_map/finish/pallas_call | solution.py:255
  (11 shorter events, 0.0 us)
Async XLA Ops:
  0.6 27.8 %copy-start = (bf16[2,64,2048]{2,1,0:T(8,128)(2,1)S(1)}, bf16[2,64,2048]{2,1,0:T(8,128)(2,1)}, u32[]{:S(2)}) copy-start(bf16[2,64,2048]{2,1,0:T(8,128)(2,1)} %refs_8_.3) | copy-start | bytes 1572868
  1.6 7.6 %collective-permute-start.1 = (f32[64,256]{1,0:T(8,128)S(1)}, f32[64,256]{1,0:T(8,128)S(1)}, u32[]{:S(2)}, u32[]{:S(2)}) collective-permute-start(f32[64,256]{1,0:T(8,128)S(1)} %pack.1), channel_id=1, source_target_pairs={{0,24},{1,25},{2,26},{3,27},{4,28},{5,29},{6,30},{7,31},{8,16},{9,... | collective-permute-start | bytes 196616 | tf_op jit(solution)/shard_map/ppermute | solution.py:33
  6.8 5.6 %collective-permute-start = (f32[64,256]{1,0:T(8,128)S(1)}, f32[64,256]{1,0:T(8,128)S(1)}, u32[]{:S(2)}, u32[]{:S(2)}) collective-permute-start(f32[64,256]{1,0:T(8,128)S(1)} %pack.1), channel_id=1, source_target_pairs={{0,16},{1,17},{2,18},{3,19},{4,20},{5,21},{6,22},{7,23},{8,24},{9,... | collective-permute-start | bytes 196616 | tf_op jit(solution)/shard_map/ppermute | solution.py:33
  6.8 8.6 %collective-permute-start.9 = (f32[64,256]{1,0:T(8,128)S(1)}, f32[64,256]{1,0:T(8,128)S(1)}, u32[]{:S(2)}, u32[]{:S(2)}) collective-permute-start(f32[64,256]{1,0:T(8,128)S(1)} %pack.1), channel_id=1, source_target_pairs={{0,8},{1,9},{2,10},{3,11},{4,12},{5,13},{6,14},{7,15},{8,0},{9,1},... | collective-permute-start | bytes 196616 | tf_op jit(solution)/shard_map/ppermute | solution.py:33
  12.4 6.6 %collective-permute-start.7 = (f32[2,64,256]{2,1,0:T(8,128)S(1)}, f32[2,64,256]{2,1,0:T(8,128)S(1)}, u32[]{:S(2)}, u32[]{:S(2)}) collective-permute-start(f32[2,64,256]{2,1,0:T(8,128)S(1)} %pad_maximum_fusion.refs_0_), channel_id=1, source_target_pairs={{0,6},{1,7},{2,4},{3,5},{4,2},{5,3},{6,0},{7,1},{8,14},{9,15},{10,... | collective-permute-start | bytes 393224 | tf_op jit(solution)/shard_map/ppermute | solution.py:33
  14.9 9.2 %collective-permute-start.5 = (f32[2,64,256]{2,1,0:T(8,128)S(1)}, f32[2,64,256]{2,1,0:T(8,128)S(1)}, u32[]{:S(2)}, u32[]{:S(2)}) collective-permute-start(f32[2,64,256]{2,1,0:T(8,128)S(1)} %pad_maximum_fusion.refs_0_), channel_id=1, source_target_pairs={{0,4},{1,5},{2,6},{3,7},{4,0},{5,1},{6,2},{7,3},{8,12},{9,13},{10,... | collective-permute-start | bytes 393224 | tf_op jit(solution)/shard_map/ppermute | solution.py:33
  15.4 13.0 %copy-start.1 = (s32[2]{0:T(128)S(1)}, s32[2]{0:T(128)}, u32[]{:S(2)}) copy-start(s32[2]{0:T(128)} %ranks.1) | copy-start | bytes 28
  15.4 8.7 %collective-permute-start.15 = (f32[2,64,256]{2,1,0:T(8,128)S(1)}, f32[2,64,256]{2,1,0:T(8,128)S(1)}, u32[]{:S(2)}, u32[]{:S(2)}) collective-permute-start(f32[2,64,256]{2,1,0:T(8,128)S(1)} %pad_maximum_fusion.1.refs_0_), channel_id=1, source_target_pairs={{0,6},{1,7},{2,4},{3,5},{4,2},{5,3},{6,0},{7,1},{8,14},{9,15},{10,... | collective-permute-start | bytes 393224 | tf_op jit(solution)/shard_map/ppermute | solution.py:33
  17.0 9.9 %collective-permute-start.13 = (f32[2,64,256]{2,1,0:T(8,128)S(1)}, f32[2,64,256]{2,1,0:T(8,128)S(1)}, u32[]{:S(2)}, u32[]{:S(2)}) collective-permute-start(f32[2,64,256]{2,1,0:T(8,128)S(1)} %pad_maximum_fusion.1.refs_0_), channel_id=1, source_target_pairs={{0,4},{1,5},{2,6},{3,7},{4,0},{5,1},{6,2},{7,3},{8,12},{9,13},{10,... | collective-permute-start | bytes 393224 | tf_op jit(solution)/shard_map/ppermute | solution.py:33
  17.5 9.4 %collective-permute-start.11 = (f32[2,64,256]{2,1,0:T(8,128)S(1)}, f32[2,64,256]{2,1,0:T(8,128)S(1)}, u32[]{:S(2)}, u32[]{:S(2)}) collective-permute-start(f32[2,64,256]{2,1,0:T(8,128)S(1)} %pad_maximum_fusion.1.refs_0_), channel_id=1, source_target_pairs={{0,2},{1,3},{2,0},{3,1},{4,6},{5,7},{6,4},{7,5},{8,10},{9,11},{10,... | collective-permute-start | bytes 393224 | tf_op jit(solution)/shard_map/ppermute | solution.py:33
  19.0 8.4 %collective-permute-start.3 = (f32[2,64,256]{2,1,0:T(8,128)S(1)}, f32[2,64,256]{2,1,0:T(8,128)S(1)}, u32[]{:S(2)}, u32[]{:S(2)}) collective-permute-start(f32[2,64,256]{2,1,0:T(8,128)S(1)} %pad_maximum_fusion.refs_0_), channel_id=1, source_target_pairs={{0,2},{1,3},{2,0},{3,1},{4,6},{5,7},{6,4},{7,5},{8,10},{9,11},{10,... | collective-permute-start | bytes 393224 | tf_op jit(solution)/shard_map/ppermute | solution.py:33
  24.1 3.3 %collective-permute-start.10 = (f32[2,64,256]{2,1,0:T(8,128)S(1)}, f32[2,64,256]{2,1,0:T(8,128)S(1)}, u32[]{:S(2)}, u32[]{:S(2)}) collective-permute-start(f32[2,64,256]{2,1,0:T(8,128)S(1)} %pad_maximum_fusion.1.refs_0_), channel_id=1, source_target_pairs={{0,1},{1,0},{2,3},{3,2},{4,5},{5,4},{6,7},{7,6},{8,9},{9,8},{10,11... | collective-permute-start | bytes 393224 | tf_op jit(solution)/shard_map/ppermute | solution.py:33
  24.1 3.7 %collective-permute-start.16 = (f32[2,64,256]{2,1,0:T(8,128)S(1)}, f32[2,64,256]{2,1,0:T(8,128)S(1)}, u32[]{:S(2)}, u32[]{:S(2)}) collective-permute-start(f32[2,64,256]{2,1,0:T(8,128)S(1)} %collective-permute-done.15.refs_6_), channel_id=1, source_target_pairs={{0,1},{1,0},{2,3},{3,2},{4,5},{5,4},{6,7},{7,6},{8,9},{9,8},{10,11... | collective-permute-start | bytes 393224 | tf_op jit(solution)/shard_map/ppermute | solution.py:33
  26.9 1.3 %collective-permute-start.14 = (f32[2,64,256]{2,1,0:T(8,128)S(1)}, f32[2,64,256]{2,1,0:T(8,128)S(1)}, u32[]{:S(2)}, u32[]{:S(2)}) collective-permute-start(f32[2,64,256]{2,1,0:T(8,128)S(1)} %collective-permute-done.13.refs_4_), channel_id=1, source_target_pairs={{0,1},{1,0},{2,3},{3,2},{4,5},{5,4},{6,7},{7,6},{8,9},{9,8},{10,11... | collective-permute-start | bytes 393224 | tf_op jit(solution)/shard_map/ppermute | solution.py:33
  26.9 1.5 %collective-permute-start.12 = (f32[2,64,256]{2,1,0:T(8,128)S(1)}, f32[2,64,256]{2,1,0:T(8,128)S(1)}, u32[]{:S(2)}, u32[]{:S(2)}) collective-permute-start(f32[2,64,256]{2,1,0:T(8,128)S(1)} %collective-permute-done.11.refs_2_), channel_id=1, source_target_pairs={{0,1},{1,0},{2,3},{3,2},{4,5},{5,4},{6,7},{7,6},{8,9},{9,8},{10,11... | collective-permute-start | bytes 393224 | tf_op jit(solution)/shard_map/ppermute | solution.py:33
  27.4 3.3 %collective-permute-start.2 = (f32[2,64,256]{2,1,0:T(8,128)S(1)}, f32[2,64,256]{2,1,0:T(8,128)S(1)}, u32[]{:S(2)}, u32[]{:S(2)}) collective-permute-start(f32[2,64,256]{2,1,0:T(8,128)S(1)} %pad_maximum_fusion.refs_0_), channel_id=1, source_target_pairs={{0,1},{1,0},{2,3},{3,2},{4,5},{5,4},{6,7},{7,6},{8,9},{9,8},{10,11... | collective-permute-start | bytes 393224 | tf_op jit(solution)/shard_map/ppermute | solution.py:33
  27.4 3.3 %collective-permute-start.8 = (f32[2,64,256]{2,1,0:T(8,128)S(1)}, f32[2,64,256]{2,1,0:T(8,128)S(1)}, u32[]{:S(2)}, u32[]{:S(2)}) collective-permute-start(f32[2,64,256]{2,1,0:T(8,128)S(1)} %collective-permute-done.7.refs_6_), channel_id=1, source_target_pairs={{0,1},{1,0},{2,3},{3,2},{4,5},{5,4},{6,7},{7,6},{8,9},{9,8},{10,11... | collective-permute-start | bytes 393224 | tf_op jit(solution)/shard_map/ppermute | solution.py:33
  27.9 2.8 %collective-permute-start.6 = (f32[2,64,256]{2,1,0:T(8,128)S(1)}, f32[2,64,256]{2,1,0:T(8,128)S(1)}, u32[]{:S(2)}, u32[]{:S(2)}) collective-permute-start(f32[2,64,256]{2,1,0:T(8,128)S(1)} %collective-permute-done.5.refs_4_), channel_id=1, source_target_pairs={{0,1},{1,0},{2,3},{3,2},{4,5},{5,4},{6,7},{7,6},{8,9},{9,8},{10,11... | collective-permute-start | bytes 393224 | tf_op jit(solution)/shard_map/ppermute | solution.py:33
  28.2 2.5 %collective-permute-start.4 = (f32[2,64,256]{2,1,0:T(8,128)S(1)}, f32[2,64,256]{2,1,0:T(8,128)S(1)}, u32[]{:S(2)}, u32[]{:S(2)}) collective-permute-start(f32[2,64,256]{2,1,0:T(8,128)S(1)} %collective-permute-done.3.refs_2_), channel_id=1, source_target_pairs={{0,1},{1,0},{2,3},{3,2},{4,5},{5,4},{6,7},{7,6},{8,9},{9,8},{10,11... | collective-permute-start | bytes 393224 | tf_op jit(solution)/shard_map/ppermute | solution.py:33

commit v4 on v3

--- a/solution.py
+++ b/solution.py
@@ -9,7 +9,7 @@
 
 
 AXIS = "blk"
-PARTS = 2
+PARTS = 1
 F32 = jnp.float32
 BF16 = jnp.bfloat16
 VMEM = pl.BlockSpec(memory_space=pltpu.VMEM)
@@ -142,34 +142,32 @@
     return cross, dot(jnp.concatenate([high, low], axis=0), other[...])
 
 
-def first_kernel(masks, ranks, *refs):
-    count = len(masks)
-    pieces = refs[:count]
-    right, inverse, left, side = refs[count : count + 4]
-    sums_out, cross_out, solved_out, keep_out, inverse_out, left_out, side_out = refs[count + 4 : count + 11]
-    both, other, sems = refs[count + 11 :]
+def load_kernel(kmax, ranks, inverse, left, side, keep, inverse_out, left_out, side_out, sems):
     pairs = ((inverse, inverse_out), (left, left_out), (side, side_out))
     copies = [pltpu.make_async_copy(hbm, out, sems.at[at]) for at, (hbm, out) in enumerate(pairs)]
     for copy in copies:
         copy.start()
-    tiles, kmax, _ = right.shape
-    for tile in range(tiles):
-        at = pl.ds(tile * kmax, kmax)
-        row = lax.broadcasted_iota(jnp.int32, (kmax, keep_out.shape[1]), 0)
-        keep_out[at, :] = (row < ranks[tile]).astype(F32)
+    for tile in range(keep.shape[0] // kmax):
+        row = lax.broadcasted_iota(jnp.int32, (kmax, keep.shape[1]), 0)
+        keep[pl.ds(tile * kmax, kmax), :] = (row < ranks[tile]).astype(F32)
+    for copy in copies:
+        copy.wait()
+
+
+def first_kernel(masks, *refs):
+    count = len(masks)
+    pieces = refs[:count]
+    right, inverse, sums_out, cross_out, solved_out, both, other = refs[count:]
     fill(pieces, masks, both, 0)
     fill(pieces, masks, other, both.shape[1] // 2)
     sums_out[...] = panel_product(pieces, masks, 0, right, both)
-    copies[0].wait()
-    cross_out[...], solved_out[...] = pivot_products(pieces, masks, 0, inverse_out, both, other)
-    for copy in copies[1:]:
-        copy.wait()
+    cross_out[...], solved_out[...] = pivot_products(pieces, masks, 0, inverse, both, other)
 
 
 def finish_kernel(masks, *refs):
     count = len(masks)
     pieces = refs[:count]
-    right, sums_in, cross_in, solved_in, keep, inverse, left, side = refs[count : count + 8]
+    right, keep, sums_in, cross_in, solved_in, inverse, left, side = refs[count : count + 8]
     new_left, new_rhs, solution_out = refs[count + 8 : count + 11]
     both, other, left_buf, rhs_buf, solution_buf, sems = refs[count + 11 :]
     tiles, kmax, places = left.shape
@@ -194,12 +192,19 @@
     for tile in range(tiles):
         mine = sums[tile * kmax : (tile + 1) * kmax]
         high, low = split(mine[:, half:wide] + mine[:, wide + half :])
-        weights = jnp.concatenate([mine[:, :half].astype(BF16), high, low], axis=1)
+        gram = mine[:, :half].astype(BF16)
+        weights = jnp.concatenate(
+            [
+                jnp.concatenate([gram, high], axis=1),
+                jnp.concatenate([jnp.zeros_like(gram), low], axis=1),
+            ],
+            axis=0,
+        )
         for part in range(PARTS):
             at = (tile, slice(None), pl.ds(part * span, span))
-            product = dot_rows(weights, left[at])
+            product = dot_rows(weights, jnp.concatenate([left[at], left[at]], axis=0))
             left_buf[at] = product[:half].astype(BF16)
-            rhs_buf[at] = side[at] - (product[half:wide] + product[wide:])
+            rhs_buf[at] = side[at] - product[half:]
             for buf, hbm in ((left_buf, new_left), (rhs_buf, new_rhs)):
                 copy = pltpu.make_async_copy(buf.at[at], hbm.at[at], sems.at[len(copies)])
                 copy.start()
@@ -217,7 +222,7 @@
     nrhs = finished.shape[1]
     width = 2 * (cols + nrhs)
     params = pltpu.CompilerParams(vmem_limit_bytes=20 * 1024 * 1024)
-    first_params = pltpu.CompilerParams(vmem_limit_bytes=52_000_000)
+    load_params = pltpu.CompilerParams(vmem_limit_bytes=56_000_000)
     block = pl.pallas_call(
         pack_kernel,
         out_shape=pltpu.VMEM((rows, width), F32),
@@ -233,6 +238,20 @@
         name="pack",
     )(pivot_right, finished, pivot_left, pivot_rhs)
     near, far = gather_halves(block, count)
+    keep, inverse, left, side = pl.pallas_call(
+        functools.partial(load_kernel, kmax),
+        out_shape=(
+            pltpu.VMEM((tiles * kmax, width), F32),
+            pltpu.VMEM(diag_inverse.shape, F32),
+            pltpu.VMEM(panel_left.shape, BF16),
+            pltpu.VMEM(rhs.shape, F32),
+        ),
+        in_specs=[pl.BlockSpec(memory_space=pltpu.SMEM)] + [HBM] * 3,
+        out_specs=(VMEM,) * 4,
+        scratch_shapes=[pltpu.SemaphoreType.DMA((3,))],
+        compiler_params=load_params,
+        name="load",
+    )(ranks, diag_inverse, panel_left, rhs)
     halves = [pltpu.VMEM((places // 2, width), BF16)] * 2
     middle = pl.pallas_call(
         functools.partial(first_kernel, [mask for _, mask in near]),
@@ -240,18 +259,14 @@
             pltpu.VMEM((tiles * kmax, width), F32),
             pltpu.VMEM((cols, width), F32),
             pltpu.VMEM((2 * rows, width), F32),
-            pltpu.VMEM((tiles * kmax, width), F32),
-            pltpu.VMEM(diag_inverse.shape, F32),
-            pltpu.VMEM(panel_left.shape, BF16),
-            pltpu.VMEM(rhs.shape, F32),
         ),
-        in_specs=[pl.BlockSpec(memory_space=pltpu.SMEM)] + [VMEM] * (len(near) + 1) + [HBM] * 3,
-        out_specs=(VMEM,) * 7,
-        scratch_shapes=halves + [pltpu.SemaphoreType.DMA((3,))],
-        compiler_params=first_params,
+        in_specs=[VMEM] * (len(near) + 2),
+        out_specs=(VMEM,) * 3,
+        scratch_shapes=halves,
+        compiler_params=params,
         cost_estimate=pl.CostEstimate(flops=300_000_000, bytes_accessed=4_000_000, transcendentals=0),
         name="first",
-    )(ranks, *[piece for piece, _ in near], panel_right, diag_inverse, panel_left, rhs)
+    )(*[piece for piece, _ in near], panel_right, inverse)
     return pl.pallas_call(
         functools.partial(finish_kernel, [mask for _, mask in far]),
         out_shape=(
@@ -270,7 +285,7 @@
         ],
         compiler_params=params,
         name="finish",
-    )(*[piece for piece, _ in far], panel_right, *middle)
+    )(*[piece for piece, _ in far], panel_right, keep, *middle, inverse, left, side)
 
 
 def solution(mesh):

time: 33.1 us -> 33.6 us (1.015)
  Pallas kernels: 5.43 us -> 5.86 us
    pallas_call x0 -> x1, Pallas kernels: none -> 2.23 us  [shards(): pl.pallas_call(functools.partial(load_kernel, kmax), out_shape=(pltpu.VME...]
    pallas_call x1, Pallas kernels: 2.29 us -> 0.54 us  [shards(): pl.pallas_call(functools.partial(first_kernel, [mask for _, mask in near]...]
  transfers between devices with their start and end apart: 17 -> 17, of which waited for: 5 -> 5; matrix products, arithmetic and copies ran while one was open for 0% -> 0% of each run, Pallas kernels for 7% -> 8%
where the time goes in v4:
time: 33.6 us; the launch traced here: 33.3 us
  starting transfers between devices  16.5 us (49%)
  waiting for transfers between devices  10.3 us (31%)
  Pallas kernels  5.86 us (17%)
  between operations  0.73 us (2%)
    ppermute x17, starting transfers between devices, swap(): return lax.ppermute(block, AXIS, [(i, i ^ mask) for i in range(count)])  16.5 us
    ppermute x17, waiting for transfers between devices, swap(): return lax.ppermute(block, AXIS, [(i, i ^ mask) for i in range(count)])  10.3 us
    pallas_call x1, Pallas kernels, shards(): pl.pallas_call(functools.partial(load_kernel, kmax), out_shape=(pltpu.VME...  2.23 us
    pallas_call x1, Pallas kernels, shards(): pl.pallas_call(functools.partial(finish_kernel, [mask for _, mask in far]...  2.16 us
    pallas_call x1, Pallas kernels, shards(): pl.pallas_call(pack_kernel, out_shape=pltpu.VMEM((rows, width), F32), in_...  0.93 us
  transfers between devices with their start and end apart: 17, of which 5 were waited for; matrix products, arithmetic and copies ran while one was open for 0% of the time, Pallas kernels for 8%

profile of v4, /device:TPU:0, one launch (start us, length us, event | category | flops | bytes accessed | tf_op | source)
XLA Modules:
  0.0 33.3 jit_solution(17240990009789413176)
XLA Ops:
  0.6 0.9 %pack.1 = f32[64,256]{1,0:T(8,128)S(1)} custom-call(bf16[64,64]{1,0:T(8,128)(2,1)} %right.1, f32[64,64]{1,0:T(8,128)} %done.1, bf16[64,64]{1,0:T(8,128)(2,1)} %left.2, f32[64,64]{1,0:T(8,128)} %side.2), custom_call_target="tpu_custom_call" | custom-call | tf_op jit(solution)/shard_map/pack/pallas_call | solution.py:226
  1.6 5.1 %collective-permute-start.1 = (f32[64,256]{1,0:T(8,128)S(1)}, f32[64,256]{1,0:T(8,128)S(1)}, u32[]{:S(2)}, u32[]{:S(2)}) collective-permute-start(f32[64,256]{1,0:T(8,128)S(1)} %pack.1), channel_id=1, source_target_pairs={{0,24},{1,25},{2,26},{3,27},{4,28},{5,29},{6,30},{7,31},{8,16},{9,... | collective-permute-start | bytes 196616 | tf_op jit(solution)/shard_map/ppermute | solution.py:33
  6.7 0.6 %collective-permute-start.9 = (f32[64,256]{1,0:T(8,128)S(1)}, f32[64,256]{1,0:T(8,128)S(1)}, u32[]{:S(2)}, u32[]{:S(2)}) collective-permute-start(f32[64,256]{1,0:T(8,128)S(1)} %pack.1), channel_id=1, source_target_pairs={{0,8},{1,9},{2,10},{3,11},{4,12},{5,13},{6,14},{7,15},{8,0},{9,1},... | collective-permute-start | bytes 196616 | tf_op jit(solution)/shard_map/ppermute | solution.py:33
  7.4 1.8 %collective-permute-done.1 = f32[64,256]{1,0:T(8,128)S(1)} collective-permute-done((f32[64,256]{1,0:T(8,128)S(1)}, f32[64,256]{1,0:T(8,128)S(1)}, u32[]{:S(2)}, u32[]{:S(2)}) %collective-permute-start.1) | collective-permute-done | bytes 65568 | tf_op jit(solution)/shard_map/ppermute | solution.py:33
  9.2 3.1 %collective-permute-done = f32[64,256]{1,0:T(8,128)S(1)} collective-permute-done((f32[64,256]{1,0:T(8,128)S(1)}, f32[64,256]{1,0:T(8,128)S(1)}, u32[]{:S(2)}, u32[]{:S(2)}) %collective-permute-start) | collective-permute-done | bytes 65568 | tf_op jit(solution)/shard_map/ppermute | solution.py:33
  12.3 2.5 %collective-permute-start.7 = (f32[2,64,256]{2,1,0:T(8,128)S(1)}, f32[2,64,256]{2,1,0:T(8,128)S(1)}, u32[]{:S(2)}, u32[]{:S(2)}) collective-permute-start(f32[2,64,256]{2,1,0:T(8,128)S(1)} %pad_maximum_fusion.refs_0_), channel_id=1, source_target_pairs={{0,6},{1,7},{2,4},{3,5},{4,2},{5,3},{6,0},{7,1},{8,14},{9,15},{10,... | collective-permute-start | bytes 393224 | tf_op jit(solution)/shard_map/ppermute | solution.py:33
  14.8 0.5 %collective-permute-start.5 = (f32[2,64,256]{2,1,0:T(8,128)S(1)}, f32[2,64,256]{2,1,0:T(8,128)S(1)}, u32[]{:S(2)}, u32[]{:S(2)}) collective-permute-start(f32[2,64,256]{2,1,0:T(8,128)S(1)} %pad_maximum_fusion.refs_0_), channel_id=1, source_target_pairs={{0,4},{1,5},{2,6},{3,7},{4,0},{5,1},{6,2},{7,3},{8,12},{9,13},{10,... | collective-permute-start | bytes 393224 | tf_op jit(solution)/shard_map/ppermute | solution.py:33
  15.4 0.0 copy-start
  15.4 1.6 %collective-permute-start.15 = (f32[2,64,256]{2,1,0:T(8,128)S(1)}, f32[2,64,256]{2,1,0:T(8,128)S(1)}, u32[]{:S(2)}, u32[]{:S(2)}) collective-permute-start(f32[2,64,256]{2,1,0:T(8,128)S(1)} %pad_maximum_fusion.1.refs_0_), channel_id=1, source_target_pairs={{0,6},{1,7},{2,4},{3,5},{4,2},{5,3},{6,0},{7,1},{8,14},{9,15},{10,... | collective-permute-start | bytes 393224 | tf_op jit(solution)/shard_map/ppermute | solution.py:33
  16.9 0.5 %collective-permute-start.13 = (f32[2,64,256]{2,1,0:T(8,128)S(1)}, f32[2,64,256]{2,1,0:T(8,128)S(1)}, u32[]{:S(2)}, u32[]{:S(2)}) collective-permute-start(f32[2,64,256]{2,1,0:T(8,128)S(1)} %pad_maximum_fusion.1.refs_0_), channel_id=1, source_target_pairs={{0,4},{1,5},{2,6},{3,7},{4,0},{5,1},{6,2},{7,3},{8,12},{9,13},{10,... | collective-permute-start | bytes 393224 | tf_op jit(solution)/shard_map/ppermute | solution.py:33
  17.4 1.5 %collective-permute-start.11 = (f32[2,64,256]{2,1,0:T(8,128)S(1)}, f32[2,64,256]{2,1,0:T(8,128)S(1)}, u32[]{:S(2)}, u32[]{:S(2)}) collective-permute-start(f32[2,64,256]{2,1,0:T(8,128)S(1)} %pad_maximum_fusion.1.refs_0_), channel_id=1, source_target_pairs={{0,2},{1,3},{2,0},{3,1},{4,6},{5,7},{6,4},{7,5},{8,10},{9,11},{10,... | collective-permute-start | bytes 393224 | tf_op jit(solution)/shard_map/ppermute | solution.py:33
  18.9 0.0 collective-permute-done.7.refs_6_
  18.9 2.3 %collective-permute-start.3 = (f32[2,64,256]{2,1,0:T(8,128)S(1)}, f32[2,64,256]{2,1,0:T(8,128)S(1)}, u32[]{:S(2)}, u32[]{:S(2)}) collective-permute-start(f32[2,64,256]{2,1,0:T(8,128)S(1)} %pad_maximum_fusion.refs_0_), channel_id=1, source_target_pairs={{0,2},{1,3},{2,0},{3,1},{4,6},{5,7},{6,4},{7,5},{8,10},{9,11},{10,... | collective-permute-start | bytes 393224 | tf_op jit(solution)/shard_map/ppermute | solution.py:33
  21.2 2.8 %collective-permute-done.5.refs_4_ = f32[2,64,256]{2,1,0:T(8,128)S(1)} collective-permute-done((f32[2,64,256]{2,1,0:T(8,128)S(1)}, f32[2,64,256]{2,1,0:T(8,128)S(1)}, u32[]{:S(2)}, u32[]{:S(2)}) %collective-permute-start.5) | collective-permute-done | bytes 131104 | tf_op jit(solution)/shard_map/ppermute | solution.py:33
  24.1 0.5 %collective-permute-start.16 = (f32[2,64,256]{2,1,0:T(8,128)S(1)}, f32[2,64,256]{2,1,0:T(8,128)S(1)}, u32[]{:S(2)}, u32[]{:S(2)}) collective-permute-start(f32[2,64,256]{2,1,0:T(8,128)S(1)} %collective-permute-done.15.refs_6_), channel_id=1, source_target_pairs={{0,1},{1,0},{2,3},{3,2},{4,5},{5,4},{6,7},{7,6},{8,9},{9,8},{10,11... | collective-permute-start | bytes 393224 | tf_op jit(solution)/shard_map/ppermute | solution.py:33
  24.6 2.2 %collective-permute-done.13.refs_4_ = f32[2,64,256]{2,1,0:T(8,128)S(1)} collective-permute-done((f32[2,64,256]{2,1,0:T(8,128)S(1)}, f32[2,64,256]{2,1,0:T(8,128)S(1)}, u32[]{:S(2)}, u32[]{:S(2)}) %collective-permute-start.13) | collective-permute-done | bytes 131104 | tf_op jit(solution)/shard_map/ppermute | solution.py:33
  26.8 0.0 collective-permute-start.14
  26.8 0.0 collective-permute-done.11.refs_2_
  26.8 0.5 %collective-permute-start.12 = (f32[2,64,256]{2,1,0:T(8,128)S(1)}, f32[2,64,256]{2,1,0:T(8,128)S(1)}, u32[]{:S(2)}, u32[]{:S(2)}) collective-permute-start(f32[2,64,256]{2,1,0:T(8,128)S(1)} %collective-permute-done.11.refs_2_), channel_id=1, source_target_pairs={{0,1},{1,0},{2,3},{3,2},{4,5},{5,4},{6,7},{7,6},{8,9},{9,8},{10,11... | collective-permute-start | bytes 393224 | tf_op jit(solution)/shard_map/ppermute | solution.py:33
  27.3 0.0 collective-permute-done.3.refs_2_
  27.3 0.1 collective-permute-start.2
  27.4 0.0 collective-permute-done.10.refs_1_
  27.4 0.4 %collective-permute-start.8 = (f32[2,64,256]{2,1,0:T(8,128)S(1)}, f32[2,64,256]{2,1,0:T(8,128)S(1)}, u32[]{:S(2)}, u32[]{:S(2)}) collective-permute-start(f32[2,64,256]{2,1,0:T(8,128)S(1)} %collective-permute-done.7.refs_6_), channel_id=1, source_target_pairs={{0,1},{1,0},{2,3},{3,2},{4,5},{5,4},{6,7},{7,6},{8,9},{9,8},{10,11... | collective-permute-start | bytes 393224 | tf_op jit(solution)/shard_map/ppermute | solution.py:33
  27.8 0.0 collective-permute-done.16.refs_7_
  27.8 0.1 collective-permute-start.6
  27.9 0.2 collective-permute-done.14.refs_5_
  28.1 0.2 collective-permute-start.4
  28.3 2.2 %load.1 = (f32[128,256]{1,0:T(8,128)S(1)}, f32[64,2048]{1,0:T(8,128)S(1)}, bf16[2,64,2048]{2,1,0:T(8,128)(2,1)S(1)}, f32[2,64,2048]{2,1,0:T(8,128)S(1)}) custom-call(s32[2]{0:T(128)} %ranks.1, f32[64,2048]{1,0:T(8,128)} %inverse.1, bf16[2,64,2048]{2,1,0:T(8,128)(2,1)} %left.3, f32[2,64,2048]{2,1,0:T(8,128)} %side.3), custom_call_target="tpu_custom_call" | custom-call | tf_op jit(solution)/shard_map/load/pallas_call | solution.py:241
  30.6 0.0 collective-permute-done.12.refs_3_
  30.6 0.5 %first.1 = (f32[128,256]{1,0:T(8,128)S(1)}, f32[64,256]{1,0:T(8,128)S(1)}, f32[128,256]{1,0:T(8,128)S(1)}) custom-call(f32[2,64,256]{2,1,0:T(8,128)S(1)} %pad_maximum_fusion.1.refs_0_, f32[2,64,256]{2,1,0:T(8,128)S(1)} %collective-permute-done.10.refs_1_, f32[2,64,256]{2,1,0:T(8,128)S(1)} %collective-permute-done.11.refs_2_, ...), custom_call_target="tpu_custom_call" | custom-call | flops 300000000 | bytes 4000000 | tf_op jit(solution)/shard_map/first/pallas_call | solution.py:256
  31.1 0.0 collective-permute-done.2.refs_1_
  31.2 2.2 %finish.1 = (bf16[2,64,2048]{2,1,0:T(8,128)(2,1)}, f32[2,64,2048]{2,1,0:T(8,128)}, f32[64,64]{1,0:T(8,128)}) custom-call(f32[2,64,256]{2,1,0:T(8,128)S(1)} %pad_maximum_fusion.refs_0_, f32[2,64,256]{2,1,0:T(8,128)S(1)} %collective-permute-done.2.refs_1_, f32[2,64,256]{2,1,0:T(8,128)S(1)} %collective-permute-done.3.refs_2_, ...), custom_call_target="tpu_custom_call" | custom-call | tf_op jit(solution)/shard_map/finish/pallas_call | solution.py:270
  (10 shorter events, 0.0 us)
Async XLA Ops:
  1.6 7.6 %collective-permute-start.1 = (f32[64,256]{1,0:T(8,128)S(1)}, f32[64,256]{1,0:T(8,128)S(1)}, u32[]{:S(2)}, u32[]{:S(2)}) collective-permute-start(f32[64,256]{1,0:T(8,128)S(1)} %pack.1), channel_id=1, source_target_pairs={{0,24},{1,25},{2,26},{3,27},{4,28},{5,29},{6,30},{7,31},{8,16},{9,... | collective-permute-start | bytes 196616 | tf_op jit(solution)/shard_map/ppermute | solution.py:33
  6.7 5.6 %collective-permute-start = (f32[64,256]{1,0:T(8,128)S(1)}, f32[64,256]{1,0:T(8,128)S(1)}, u32[]{:S(2)}, u32[]{:S(2)}) collective-permute-start(f32[64,256]{1,0:T(8,128)S(1)} %pack.1), channel_id=1, source_target_pairs={{0,16},{1,17},{2,18},{3,19},{4,20},{5,21},{6,22},{7,23},{8,24},{9,... | collective-permute-start | bytes 196616 | tf_op jit(solution)/shard_map/ppermute | solution.py:33
  6.7 8.6 %collective-permute-start.9 = (f32[64,256]{1,0:T(8,128)S(1)}, f32[64,256]{1,0:T(8,128)S(1)}, u32[]{:S(2)}, u32[]{:S(2)}) collective-permute-start(f32[64,256]{1,0:T(8,128)S(1)} %pack.1), channel_id=1, source_target_pairs={{0,8},{1,9},{2,10},{3,11},{4,12},{5,13},{6,14},{7,15},{8,0},{9,1},... | collective-permute-start | bytes 196616 | tf_op jit(solution)/shard_map/ppermute | solution.py:33
  12.3 6.6 %collective-permute-start.7 = (f32[2,64,256]{2,1,0:T(8,128)S(1)}, f32[2,64,256]{2,1,0:T(8,128)S(1)}, u32[]{:S(2)}, u32[]{:S(2)}) collective-permute-start(f32[2,64,256]{2,1,0:T(8,128)S(1)} %pad_maximum_fusion.refs_0_), channel_id=1, source_target_pairs={{0,6},{1,7},{2,4},{3,5},{4,2},{5,3},{6,0},{7,1},{8,14},{9,15},{10,... | collective-permute-start | bytes 393224 | tf_op jit(solution)/shard_map/ppermute | solution.py:33
  14.8 9.2 %collective-permute-start.5 = (f32[2,64,256]{2,1,0:T(8,128)S(1)}, f32[2,64,256]{2,1,0:T(8,128)S(1)}, u32[]{:S(2)}, u32[]{:S(2)}) collective-permute-start(f32[2,64,256]{2,1,0:T(8,128)S(1)} %pad_maximum_fusion.refs_0_), channel_id=1, source_target_pairs={{0,4},{1,5},{2,6},{3,7},{4,0},{5,1},{6,2},{7,3},{8,12},{9,13},{10,... | collective-permute-start | bytes 393224 | tf_op jit(solution)/shard_map/ppermute | solution.py:33
  15.4 15.2 %copy-start = (bf16[2,64,2048]{2,1,0:T(8,128)(2,1)S(1)}, bf16[2,64,2048]{2,1,0:T(8,128)(2,1)}, u32[]{:S(2)}) copy-start(bf16[2,64,2048]{2,1,0:T(8,128)(2,1)} %refs_8_.3) | copy-start | bytes 1572868
  15.4 8.7 %collective-permute-start.15 = (f32[2,64,256]{2,1,0:T(8,128)S(1)}, f32[2,64,256]{2,1,0:T(8,128)S(1)}, u32[]{:S(2)}, u32[]{:S(2)}) collective-permute-start(f32[2,64,256]{2,1,0:T(8,128)S(1)} %pad_maximum_fusion.1.refs_0_), channel_id=1, source_target_pairs={{0,6},{1,7},{2,4},{3,5},{4,2},{5,3},{6,0},{7,1},{8,14},{9,15},{10,... | collective-permute-start | bytes 393224 | tf_op jit(solution)/shard_map/ppermute | solution.py:33
  16.9 9.9 %collective-permute-start.13 = (f32[2,64,256]{2,1,0:T(8,128)S(1)}, f32[2,64,256]{2,1,0:T(8,128)S(1)}, u32[]{:S(2)}, u32[]{:S(2)}) collective-permute-start(f32[2,64,256]{2,1,0:T(8,128)S(1)} %pad_maximum_fusion.1.refs_0_), channel_id=1, source_target_pairs={{0,4},{1,5},{2,6},{3,7},{4,0},{5,1},{6,2},{7,3},{8,12},{9,13},{10,... | collective-permute-start | bytes 393224 | tf_op jit(solution)/shard_map/ppermute | solution.py:33
  17.4 9.4 %collective-permute-start.11 = (f32[2,64,256]{2,1,0:T(8,128)S(1)}, f32[2,64,256]{2,1,0:T(8,128)S(1)}, u32[]{:S(2)}, u32[]{:S(2)}) collective-permute-start(f32[2,64,256]{2,1,0:T(8,128)S(1)} %pad_maximum_fusion.1.refs_0_), channel_id=1, source_target_pairs={{0,2},{1,3},{2,0},{3,1},{4,6},{5,7},{6,4},{7,5},{8,10},{9,11},{10,... | collective-permute-start | bytes 393224 | tf_op jit(solution)/shard_map/ppermute | solution.py:33
  18.9 8.4 %collective-permute-start.3 = (f32[2,64,256]{2,1,0:T(8,128)S(1)}, f32[2,64,256]{2,1,0:T(8,128)S(1)}, u32[]{:S(2)}, u32[]{:S(2)}) collective-permute-start(f32[2,64,256]{2,1,0:T(8,128)S(1)} %pad_maximum_fusion.refs_0_), channel_id=1, source_target_pairs={{0,2},{1,3},{2,0},{3,1},{4,6},{5,7},{6,4},{7,5},{8,10},{9,11},{10,... | collective-permute-start | bytes 393224 | tf_op jit(solution)/shard_map/ppermute | solution.py:33
  24.1 3.3 %collective-permute-start.10 = (f32[2,64,256]{2,1,0:T(8,128)S(1)}, f32[2,64,256]{2,1,0:T(8,128)S(1)}, u32[]{:S(2)}, u32[]{:S(2)}) collective-permute-start(f32[2,64,256]{2,1,0:T(8,128)S(1)} %pad_maximum_fusion.1.refs_0_), channel_id=1, source_target_pairs={{0,1},{1,0},{2,3},{3,2},{4,5},{5,4},{6,7},{7,6},{8,9},{9,8},{10,11... | collective-permute-start | bytes 393224 | tf_op jit(solution)/shard_map/ppermute | solution.py:33
  24.1 3.7 %collective-permute-start.16 = (f32[2,64,256]{2,1,0:T(8,128)S(1)}, f32[2,64,256]{2,1,0:T(8,128)S(1)}, u32[]{:S(2)}, u32[]{:S(2)}) collective-permute-start(f32[2,64,256]{2,1,0:T(8,128)S(1)} %collective-permute-done.15.refs_6_), channel_id=1, source_target_pairs={{0,1},{1,0},{2,3},{3,2},{4,5},{5,4},{6,7},{7,6},{8,9},{9,8},{10,11... | collective-permute-start | bytes 393224 | tf_op jit(solution)/shard_map/ppermute | solution.py:33
  26.8 1.3 %collective-permute-start.14 = (f32[2,64,256]{2,1,0:T(8,128)S(1)}, f32[2,64,256]{2,1,0:T(8,128)S(1)}, u32[]{:S(2)}, u32[]{:S(2)}) collective-permute-start(f32[2,64,256]{2,1,0:T(8,128)S(1)} %collective-permute-done.13.refs_4_), channel_id=1, source_target_pairs={{0,1},{1,0},{2,3},{3,2},{4,5},{5,4},{6,7},{7,6},{8,9},{9,8},{10,11... | collective-permute-start | bytes 393224 | tf_op jit(solution)/shard_map/ppermute | solution.py:33
  26.8 3.8 %collective-permute-start.12 = (f32[2,64,256]{2,1,0:T(8,128)S(1)}, f32[2,64,256]{2,1,0:T(8,128)S(1)}, u32[]{:S(2)}, u32[]{:S(2)}) collective-permute-start(f32[2,64,256]{2,1,0:T(8,128)S(1)} %collective-permute-done.11.refs_2_), channel_id=1, source_target_pairs={{0,1},{1,0},{2,3},{3,2},{4,5},{5,4},{6,7},{7,6},{8,9},{9,8},{10,11... | collective-permute-start | bytes 393224 | tf_op jit(solution)/shard_map/ppermute | solution.py:33
  27.3 3.8 %collective-permute-start.2 = (f32[2,64,256]{2,1,0:T(8,128)S(1)}, f32[2,64,256]{2,1,0:T(8,128)S(1)}, u32[]{:S(2)}, u32[]{:S(2)}) collective-permute-start(f32[2,64,256]{2,1,0:T(8,128)S(1)} %pad_maximum_fusion.refs_0_), channel_id=1, source_target_pairs={{0,1},{1,0},{2,3},{3,2},{4,5},{5,4},{6,7},{7,6},{8,9},{9,8},{10,11... | collective-permute-start | bytes 393224 | tf_op jit(solution)/shard_map/ppermute | solution.py:33
  27.4 3.8 %collective-permute-start.8 = (f32[2,64,256]{2,1,0:T(8,128)S(1)}, f32[2,64,256]{2,1,0:T(8,128)S(1)}, u32[]{:S(2)}, u32[]{:S(2)}) collective-permute-start(f32[2,64,256]{2,1,0:T(8,128)S(1)} %collective-permute-done.7.refs_6_), channel_id=1, source_target_pairs={{0,1},{1,0},{2,3},{3,2},{4,5},{5,4},{6,7},{7,6},{8,9},{9,8},{10,11... | collective-permute-start | bytes 393224 | tf_op jit(solution)/shard_map/ppermute | solution.py:33
  27.8 3.4 %collective-permute-start.6 = (f32[2,64,256]{2,1,0:T(8,128)S(1)}, f32[2,64,256]{2,1,0:T(8,128)S(1)}, u32[]{:S(2)}, u32[]{:S(2)}) collective-permute-start(f32[2,64,256]{2,1,0:T(8,128)S(1)} %collective-permute-done.5.refs_4_), channel_id=1, source_target_pairs={{0,1},{1,0},{2,3},{3,2},{4,5},{5,4},{6,7},{7,6},{8,9},{9,8},{10,11... | collective-permute-start | bytes 393224 | tf_op jit(solution)/shard_map/ppermute | solution.py:33
  28.1 3.0 %collective-permute-start.4 = (f32[2,64,256]{2,1,0:T(8,128)S(1)}, f32[2,64,256]{2,1,0:T(8,128)S(1)}, u32[]{:S(2)}, u32[]{:S(2)}) collective-permute-start(f32[2,64,256]{2,1,0:T(8,128)S(1)} %collective-permute-done.3.refs_2_), channel_id=1, source_target_pairs={{0,1},{1,0},{2,3},{3,2},{4,5},{5,4},{6,7},{7,6},{8,9},{9,8},{10,11... | collective-permute-start | bytes 393224 | tf_op jit(solution)/shard_map/ppermute | solution.py:33

commit v5 on v4

--- a/solution.py
+++ b/solution.py
@@ -10,6 +10,7 @@
 
 AXIS = "blk"
 PARTS = 1
+CORE_GROUPS = {"near": [[3, 2, 1, 0]], "far": [[0, 3], [2, 1]]}
 F32 = jnp.float32
 BF16 = jnp.bfloat16
 VMEM = pl.BlockSpec(memory_space=pltpu.VMEM)
@@ -69,15 +70,15 @@
     steps = [step << first for step in range(4)]
     blocks = [block] + [swap(block, step << first, count) for step in range(1, 4)]
     halves = []
-    for at in (0, 2):
+    for at, name in ((0, "near"), (2, "far")):
         own = jnp.stack(blocks[at : at + 2])
-        half = []
-        for step in range(4):
-            mask = step << second
-            piece = swap(own, mask, count) if step else own
-            other = swap(piece, 1, count)
-            for core, part in ((0, piece), (1, other)):
-                half.append((part, [mask ^ core ^ plane for plane in steps[at : at + 2]]))
+        parts = [own] + [swap(own, step << second, count) for step in range(1, 4)]
+        masks = [[step << second ^ plane for plane in steps[at : at + 2]] for step in range(4)]
+        half = list(zip(parts, masks))
+        for group in CORE_GROUPS[name]:
+            sent = jnp.concatenate([parts[step] for step in group])
+            mask = [value ^ 1 for step in group for value in masks[step]]
+            half.append((swap(sent, 1, count), mask))
         halves.append(half)
     return halves
 

time: 33.6 us -> 29.2 us (0.87)
  starting transfers between devices: 16.5 us -> 13.4 us
  waiting for transfers between devices: 10.3 us -> 8.65 us
    ppermute x17 -> x12, starting transfers between devices: 16.5 us -> 13.4 us  [swap(): return lax.ppermute(block, AXIS, [(i, i ^ mask) for i in range(count)])]
    ppermute x17 -> x12, waiting for transfers between devices: 10.3 us -> 8.65 us  [swap(): return lax.ppermute(block, AXIS, [(i, i ^ mask) for i in range(count)])]
  transfers between devices with their start and end apart: 17 -> 12, of which waited for: 5 -> 5; matrix products, arithmetic and copies ran while one was open for 0% -> 0% of each run, Pallas kernels for 8% -> 10%
where the time goes in v5:
time: 29.2 us; the launch traced here: 28.9 us
  starting transfers between devices  13.4 us (46%)
  waiting for transfers between devices  8.65 us (30%)
  Pallas kernels  5.99 us (21%)
  between operations  0.79 us (3%)
    ppermute x12, starting transfers between devices, swap(): return lax.ppermute(block, AXIS, [(i, i ^ mask) for i in range(count)])  13.4 us
    ppermute x12, waiting for transfers between devices, swap(): return lax.ppermute(block, AXIS, [(i, i ^ mask) for i in range(count)])  8.65 us
    pallas_call x1, Pallas kernels, shards(): pl.pallas_call(functools.partial(load_kernel, kmax), out_shape=(pltpu.VME...  2.37 us
    pallas_call x1, Pallas kernels, shards(): pl.pallas_call(functools.partial(finish_kernel, [mask for _, mask in far]...  2.16 us
    pallas_call x1, Pallas kernels, shards(): pl.pallas_call(pack_kernel, out_shape=pltpu.VMEM((rows, width), F32), in_...  0.93 us
  transfers between devices with their start and end apart: 12, of which 5 were waited for; matrix products, arithmetic and copies ran while one was open for 0% of the time, Pallas kernels for 10%

profile of v5, /device:TPU:0, one launch (start us, length us, event | category | flops | bytes accessed | tf_op | source)
XLA Modules:
  0.0 28.9 jit_solution(1038598030538053123)
XLA Ops:
  0.6 0.9 %pack.1 = f32[64,256]{1,0:T(8,128)S(1)} custom-call(bf16[64,64]{1,0:T(8,128)(2,1)} %right.1, f32[64,64]{1,0:T(8,128)} %done.1, bf16[64,64]{1,0:T(8,128)(2,1)} %left.2, f32[64,64]{1,0:T(8,128)} %side.2), custom_call_target="tpu_custom_call" | custom-call | tf_op jit(solution)/shard_map/pack/pallas_call | solution.py:227
  1.6 3.1 %collective-permute-start.7 = (f32[64,256]{1,0:T(8,128)S(1)}, f32[64,256]{1,0:T(8,128)S(1)}, u32[]{:S(2)}, u32[]{:S(2)}) collective-permute-start(f32[64,256]{1,0:T(8,128)S(1)} %pack.1), channel_id=1, source_target_pairs={{0,8},{1,9},{2,10},{3,11},{4,12},{5,13},{6,14},{7,15},{8,0},{9,1},... | collective-permute-start | bytes 196616 | tf_op jit(solution)/shard_map/ppermute | solution.py:34
  4.7 2.5 %collective-permute-start.1 = (f32[64,256]{1,0:T(8,128)S(1)}, f32[64,256]{1,0:T(8,128)S(1)}, u32[]{:S(2)}, u32[]{:S(2)}) collective-permute-start(f32[64,256]{1,0:T(8,128)S(1)} %pack.1), channel_id=1, source_target_pairs={{0,24},{1,25},{2,26},{3,27},{4,28},{5,29},{6,30},{7,31},{8,16},{9,... | collective-permute-start | bytes 196616 | tf_op jit(solution)/shard_map/ppermute | solution.py:34
  7.2 0.1 collective-permute-start
  7.3 0.0 collective-permute-done.7
  7.3 2.6 %collective-permute-start.10 = (f32[2,64,256]{2,1,0:T(8,128)S(1)}, f32[2,64,256]{2,1,0:T(8,128)S(1)}, u32[]{:S(2)}, u32[]{:S(2)}) collective-permute-start(f32[2,64,256]{2,1,0:T(8,128)S(1)} %pad_maximum_fusion.3.refs_0_), channel_id=1, source_target_pairs={{0,6},{1,7},{2,4},{3,5},{4,2},{5,3},{6,0},{7,1},{8,14},{9,15},{10,... | collective-permute-start | bytes 393224 | tf_op jit(solution)/shard_map/ppermute | solution.py:34
  9.9 0.5 %collective-permute-start.9 = (f32[2,64,256]{2,1,0:T(8,128)S(1)}, f32[2,64,256]{2,1,0:T(8,128)S(1)}, u32[]{:S(2)}, u32[]{:S(2)}) collective-permute-start(f32[2,64,256]{2,1,0:T(8,128)S(1)} %pad_maximum_fusion.3.refs_0_), channel_id=1, source_target_pairs={{0,4},{1,5},{2,6},{3,7},{4,0},{5,1},{6,2},{7,3},{8,12},{9,13},{10,... | collective-permute-start | bytes 393224 | tf_op jit(solution)/shard_map/ppermute | solution.py:34
  10.4 0.4 %collective-permute-start.8 = (f32[2,64,256]{2,1,0:T(8,128)S(1)}, f32[2,64,256]{2,1,0:T(8,128)S(1)}, u32[]{:S(2)}, u32[]{:S(2)}) collective-permute-start(f32[2,64,256]{2,1,0:T(8,128)S(1)} %pad_maximum_fusion.3.refs_0_), channel_id=1, source_target_pairs={{0,2},{1,3},{2,0},{3,1},{4,6},{5,7},{6,4},{7,5},{8,10},{9,11},{10,... | collective-permute-start | bytes 393224 | tf_op jit(solution)/shard_map/ppermute | solution.py:34
  10.8 0.7 %collective-permute-done.1 = f32[64,256]{1,0:T(8,128)S(1)} collective-permute-done((f32[64,256]{1,0:T(8,128)S(1)}, f32[64,256]{1,0:T(8,128)S(1)}, u32[]{:S(2)}, u32[]{:S(2)}) %collective-permute-start.1) | collective-permute-done | bytes 65568 | tf_op jit(solution)/shard_map/ppermute | solution.py:34
  11.5 2.1 %collective-permute-done = f32[64,256]{1,0:T(8,128)S(1)} collective-permute-done((f32[64,256]{1,0:T(8,128)S(1)}, f32[64,256]{1,0:T(8,128)S(1)}, u32[]{:S(2)}, u32[]{:S(2)}) %collective-permute-start) | collective-permute-done | bytes 65568 | tf_op jit(solution)/shard_map/ppermute | solution.py:34
  13.6 1.6 %collective-permute-start.3 = (f32[2,64,256]{2,1,0:T(8,128)S(1)}, f32[2,64,256]{2,1,0:T(8,128)S(1)}, u32[]{:S(2)}, u32[]{:S(2)}) collective-permute-start(f32[2,64,256]{2,1,0:T(8,128)S(1)} %pad_maximum_fusion.2.refs_0_), channel_id=1, source_target_pairs={{0,4},{1,5},{2,6},{3,7},{4,0},{5,1},{6,2},{7,3},{8,12},{9,13},{10,... | collective-permute-start | bytes 393224 | tf_op jit(solution)/shard_map/ppermute | solution.py:34
  15.2 1.5 %collective-permute-start.2 = (f32[2,64,256]{2,1,0:T(8,128)S(1)}, f32[2,64,256]{2,1,0:T(8,128)S(1)}, u32[]{:S(2)}, u32[]{:S(2)}) collective-permute-start(f32[2,64,256]{2,1,0:T(8,128)S(1)} %pad_maximum_fusion.2.refs_0_), channel_id=1, source_target_pairs={{0,2},{1,3},{2,0},{3,1},{4,6},{5,7},{6,4},{7,5},{8,10},{9,11},{10,... | collective-permute-start | bytes 393224 | tf_op jit(solution)/shard_map/ppermute | solution.py:34
  16.7 0.0 collective-permute-done.10.refs_3_
  16.7 0.0 collective-permute-done.9.refs_2_
  16.7 0.0 collective-permute-done.8.refs_1_
  16.8 0.1 collective-permute-start.11
  16.9 0.8 %collective-permute-start.4 = (f32[2,64,256]{2,1,0:T(8,128)S(1)}, f32[2,64,256]{2,1,0:T(8,128)S(1)}, u32[]{:S(2)}, u32[]{:S(2)}) collective-permute-start(f32[2,64,256]{2,1,0:T(8,128)S(1)} %pad_maximum_fusion.2.refs_0_), channel_id=1, source_target_pairs={{0,6},{1,7},{2,4},{3,5},{4,2},{5,3},{6,0},{7,1},{8,14},{9,15},{10,... | collective-permute-start | bytes 393224 | tf_op jit(solution)/shard_map/ppermute | solution.py:34
  17.7 1.3 %collective-permute-done.3.refs_2_ = f32[2,64,256]{2,1,0:T(8,128)S(1)} collective-permute-done((f32[2,64,256]{2,1,0:T(8,128)S(1)}, f32[2,64,256]{2,1,0:T(8,128)S(1)}, u32[]{:S(2)}, u32[]{:S(2)}) %collective-permute-start.3) | collective-permute-done | bytes 131104 | tf_op jit(solution)/shard_map/ppermute | solution.py:34
  19.1 1.6 %collective-permute-done.2.refs_1_ = f32[2,64,256]{2,1,0:T(8,128)S(1)} collective-permute-done((f32[2,64,256]{2,1,0:T(8,128)S(1)}, f32[2,64,256]{2,1,0:T(8,128)S(1)}, u32[]{:S(2)}, u32[]{:S(2)}) %collective-permute-start.2) | collective-permute-done | bytes 131104 | tf_op jit(solution)/shard_map/ppermute | solution.py:34
  20.7 0.1 collective-permute-start.6
  20.7 2.9 %collective-permute-done.4.refs_3_ = f32[2,64,256]{2,1,0:T(8,128)S(1)} collective-permute-done((f32[2,64,256]{2,1,0:T(8,128)S(1)}, f32[2,64,256]{2,1,0:T(8,128)S(1)}, u32[]{:S(2)}, u32[]{:S(2)}) %collective-permute-start.4) | collective-permute-done | bytes 131104 | tf_op jit(solution)/shard_map/ppermute | solution.py:34
  23.7 0.0 copy-start
  23.7 0.1 collective-permute-start.5
  23.8 2.4 %load.1 = (f32[128,256]{1,0:T(8,128)S(1)}, f32[64,2048]{1,0:T(8,128)S(1)}, bf16[2,64,2048]{2,1,0:T(8,128)(2,1)S(1)}, f32[2,64,2048]{2,1,0:T(8,128)S(1)}) custom-call(s32[2]{0:T(128)} %ranks.1, f32[64,2048]{1,0:T(8,128)} %inverse.1, bf16[2,64,2048]{2,1,0:T(8,128)(2,1)} %left.3, f32[2,64,2048]{2,1,0:T(8,128)} %side.3), custom_call_target="tpu_custom_call" | custom-call | tf_op jit(solution)/shard_map/load/pallas_call | solution.py:242
  26.2 0.0 collective-permute-done.11.refs_4_
  26.2 0.0 copy-done
  26.2 0.5 %first.1 = (f32[128,256]{1,0:T(8,128)S(1)}, f32[64,256]{1,0:T(8,128)S(1)}, f32[128,256]{1,0:T(8,128)S(1)}) custom-call(f32[2,64,256]{2,1,0:T(8,128)S(1)} %pad_maximum_fusion.3.refs_0_, f32[2,64,256]{2,1,0:T(8,128)S(1)} %collective-permute-done.8.refs_1_, f32[2,64,256]{2,1,0:T(8,128)S(1)} %collective-permute-done.9.refs_2_, ...), custom_call_target="tpu_custom_call" | custom-call | flops 300000000 | bytes 4000000 | tf_op jit(solution)/shard_map/first/pallas_call | solution.py:257
  26.7 0.0 collective-permute-done.6.refs_5_
  26.7 0.0 collective-permute-done.5.refs_4_
  26.8 2.2 %finish.1 = (bf16[2,64,2048]{2,1,0:T(8,128)(2,1)}, f32[2,64,2048]{2,1,0:T(8,128)}, f32[64,64]{1,0:T(8,128)}) custom-call(f32[2,64,256]{2,1,0:T(8,128)S(1)} %pad_maximum_fusion.2.refs_0_, f32[2,64,256]{2,1,0:T(8,128)S(1)} %collective-permute-done.2.refs_1_, f32[2,64,256]{2,1,0:T(8,128)S(1)} %collective-permute-done.3.refs_2_, ...), custom_call_target="tpu_custom_call" | custom-call | tf_op jit(solution)/shard_map/finish/pallas_call | solution.py:271
  (9 shorter events, 0.1 us)
Async XLA Ops:
  1.6 5.7 %collective-permute-start.7 = (f32[64,256]{1,0:T(8,128)S(1)}, f32[64,256]{1,0:T(8,128)S(1)}, u32[]{:S(2)}, u32[]{:S(2)}) collective-permute-start(f32[64,256]{1,0:T(8,128)S(1)} %pack.1), channel_id=1, source_target_pairs={{0,8},{1,9},{2,10},{3,11},{4,12},{5,13},{6,14},{7,15},{8,0},{9,1},... | collective-permute-start | bytes 196616 | tf_op jit(solution)/shard_map/ppermute | solution.py:34
  4.7 6.9 %collective-permute-start.1 = (f32[64,256]{1,0:T(8,128)S(1)}, f32[64,256]{1,0:T(8,128)S(1)}, u32[]{:S(2)}, u32[]{:S(2)}) collective-permute-start(f32[64,256]{1,0:T(8,128)S(1)} %pack.1), channel_id=1, source_target_pairs={{0,24},{1,25},{2,26},{3,27},{4,28},{5,29},{6,30},{7,31},{8,16},{9,... | collective-permute-start | bytes 196616 | tf_op jit(solution)/shard_map/ppermute | solution.py:34
  7.2 6.4 %collective-permute-start = (f32[64,256]{1,0:T(8,128)S(1)}, f32[64,256]{1,0:T(8,128)S(1)}, u32[]{:S(2)}, u32[]{:S(2)}) collective-permute-start(f32[64,256]{1,0:T(8,128)S(1)} %pack.1), channel_id=1, source_target_pairs={{0,16},{1,17},{2,18},{3,19},{4,20},{5,21},{6,22},{7,23},{8,24},{9,... | collective-permute-start | bytes 196616 | tf_op jit(solution)/shard_map/ppermute | solution.py:34
  7.3 9.4 %collective-permute-start.10 = (f32[2,64,256]{2,1,0:T(8,128)S(1)}, f32[2,64,256]{2,1,0:T(8,128)S(1)}, u32[]{:S(2)}, u32[]{:S(2)}) collective-permute-start(f32[2,64,256]{2,1,0:T(8,128)S(1)} %pad_maximum_fusion.3.refs_0_), channel_id=1, source_target_pairs={{0,6},{1,7},{2,4},{3,5},{4,2},{5,3},{6,0},{7,1},{8,14},{9,15},{10,... | collective-permute-start | bytes 393224 | tf_op jit(solution)/shard_map/ppermute | solution.py:34
  9.9 6.8 %collective-permute-start.9 = (f32[2,64,256]{2,1,0:T(8,128)S(1)}, f32[2,64,256]{2,1,0:T(8,128)S(1)}, u32[]{:S(2)}, u32[]{:S(2)}) collective-permute-start(f32[2,64,256]{2,1,0:T(8,128)S(1)} %pad_maximum_fusion.3.refs_0_), channel_id=1, source_target_pairs={{0,4},{1,5},{2,6},{3,7},{4,0},{5,1},{6,2},{7,3},{8,12},{9,13},{10,... | collective-permute-start | bytes 393224 | tf_op jit(solution)/shard_map/ppermute | solution.py:34
  10.4 6.3 %collective-permute-start.8 = (f32[2,64,256]{2,1,0:T(8,128)S(1)}, f32[2,64,256]{2,1,0:T(8,128)S(1)}, u32[]{:S(2)}, u32[]{:S(2)}) collective-permute-start(f32[2,64,256]{2,1,0:T(8,128)S(1)} %pad_maximum_fusion.3.refs_0_), channel_id=1, source_target_pairs={{0,2},{1,3},{2,0},{3,1},{4,6},{5,7},{6,4},{7,5},{8,10},{9,11},{10,... | collective-permute-start | bytes 393224 | tf_op jit(solution)/shard_map/ppermute | solution.py:34
  13.6 5.4 %collective-permute-start.3 = (f32[2,64,256]{2,1,0:T(8,128)S(1)}, f32[2,64,256]{2,1,0:T(8,128)S(1)}, u32[]{:S(2)}, u32[]{:S(2)}) collective-permute-start(f32[2,64,256]{2,1,0:T(8,128)S(1)} %pad_maximum_fusion.2.refs_0_), channel_id=1, source_target_pairs={{0,4},{1,5},{2,6},{3,7},{4,0},{5,1},{6,2},{7,3},{8,12},{9,13},{10,... | collective-permute-start | bytes 393224 | tf_op jit(solution)/shard_map/ppermute | solution.py:34
  15.2 5.4 %collective-permute-start.2 = (f32[2,64,256]{2,1,0:T(8,128)S(1)}, f32[2,64,256]{2,1,0:T(8,128)S(1)}, u32[]{:S(2)}, u32[]{:S(2)}) collective-permute-start(f32[2,64,256]{2,1,0:T(8,128)S(1)} %pad_maximum_fusion.2.refs_0_), channel_id=1, source_target_pairs={{0,2},{1,3},{2,0},{3,1},{4,6},{5,7},{6,4},{7,5},{8,10},{9,11},{10,... | collective-permute-start | bytes 393224 | tf_op jit(solution)/shard_map/ppermute | solution.py:34
  16.8 9.4 %collective-permute-start.11 = (f32[8,64,256]{2,1,0:T(8,128)S(1)}, f32[8,64,256]{2,1,0:T(8,128)S(1)}, u32[]{:S(2)}, u32[]{:S(2)}) collective-permute-start(f32[8,64,256]{2,1,0:T(8,128)S(1)} %constant_dynamic-update-slice_fusion), channel_id=1, source_target_pairs={{0,1},{1,0},{2,3},{3,2},{4,5},{5,4},{6,7},{7,6},{8,9},{9,8},{10,11... | collective-permute-start | bytes 1572872 | tf_op jit(solution)/shard_map/ppermute | solution.py:34
  16.9 6.8 %collective-permute-start.4 = (f32[2,64,256]{2,1,0:T(8,128)S(1)}, f32[2,64,256]{2,1,0:T(8,128)S(1)}, u32[]{:S(2)}, u32[]{:S(2)}) collective-permute-start(f32[2,64,256]{2,1,0:T(8,128)S(1)} %pad_maximum_fusion.2.refs_0_), channel_id=1, source_target_pairs={{0,6},{1,7},{2,4},{3,5},{4,2},{5,3},{6,0},{7,1},{8,14},{9,15},{10,... | collective-permute-start | bytes 393224 | tf_op jit(solution)/shard_map/ppermute | solution.py:34
  20.7 6.1 %collective-permute-start.6 = (f32[4,64,256]{2,1,0:T(8,128)S(1)}, f32[4,64,256]{2,1,0:T(8,128)S(1)}, u32[]{:S(2)}, u32[]{:S(2)}) collective-permute-start(f32[4,64,256]{2,1,0:T(8,128)S(1)} %pad_maximum_fusion.1), channel_id=1, source_target_pairs={{0,1},{1,0},{2,3},{3,2},{4,5},{5,4},{6,7},{7,6},{8,9},{9,8},{10,11... | collective-permute-start | bytes 786440 | tf_op jit(solution)/shard_map/ppermute | solution.py:34
  23.7 2.5 %copy-start = (bf16[2,64,2048]{2,1,0:T(8,128)(2,1)S(1)}, bf16[2,64,2048]{2,1,0:T(8,128)(2,1)}, u32[]{:S(2)}) copy-start(bf16[2,64,2048]{2,1,0:T(8,128)(2,1)} %refs_6_.1) | copy-start | bytes 1572868
  23.7 3.0 %collective-permute-start.5 = (f32[4,64,256]{2,1,0:T(8,128)S(1)}, f32[4,64,256]{2,1,0:T(8,128)S(1)}, u32[]{:S(2)}, u32[]{:S(2)}) collective-permute-start(f32[4,64,256]{2,1,0:T(8,128)S(1)} %pad_maximum_fusion), channel_id=1, source_target_pairs={{0,1},{1,0},{2,3},{3,2},{4,5},{5,4},{6,7},{7,6},{8,9},{9,8},{10,11... | collective-permute-start | bytes 786440 | tf_op jit(solution)/shard_map/ppermute | solution.py:34

commit v6 on v5

--- a/solution.py
+++ b/solution.py
@@ -135,12 +135,13 @@
     return dot(right[:, :, pl.ds(start, length)].reshape(tiles * kmax, length), both[...])
 
 
-def pivot_products(pieces, masks, index, inverse, both, other):
-    length, width = both.shape
-    start = start_of(pieces, masks, index, length)
-    cross = dot_rows(both[:, : width // 4], both[...])
-    high, low = split(inverse[:, pl.ds(start, length)])
-    return cross, dot(jnp.concatenate([high, low], axis=0), other[...])
+def stacked(inverse, start, length):
+    high, low = split(inverse[:, pl.ds(pl.multiple_of(start, length), length)])
+    return jnp.concatenate([high, low], axis=0)
+
+
+def pivot_products(both, other, inverse):
+    return dot_rows(both[:, : both.shape[1] // 4], both[...]), dot(inverse, other[...])
 
 
 def load_kernel(kmax, ranks, inverse, left, side, keep, inverse_out, left_out, side_out, sems):
@@ -158,11 +159,14 @@
 def first_kernel(masks, *refs):
     count = len(masks)
     pieces = refs[:count]
-    right, inverse, sums_out, cross_out, solved_out, both, other = refs[count:]
+    right, inverse, sums_out, cross_out, solved_out, far_out, both, other = refs[count:]
     fill(pieces, masks, both, 0)
     fill(pieces, masks, other, both.shape[1] // 2)
     sums_out[...] = panel_product(pieces, masks, 0, right, both)
-    cross_out[...], solved_out[...] = pivot_products(pieces, masks, 0, inverse, both, other)
+    length = both.shape[0]
+    start = start_of(pieces, masks, 0, length)
+    cross_out[...], solved_out[...] = pivot_products(both, other, stacked(inverse, start, length))
+    far_out[...] = stacked(inverse, inverse.shape[1] - length - start, length)
 
 
 def finish_kernel(masks, *refs):
@@ -177,7 +181,7 @@
     fill(pieces, masks, both, 0)
     sums = (panel_product(pieces, masks, 1, right, both) + sums_in[...]) * keep[...]
     fill(pieces, masks, other, wide)
-    cross, solved = pivot_products(pieces, masks, 1, inverse, both, other)
+    cross, solved = pivot_products(both, other, inverse[...])
     cross += cross_in[...]
     solved += solved_in[...]
     high, low = split(cross[:, half:wide] + cross[:, wide + half :])
@@ -260,9 +264,10 @@
             pltpu.VMEM((tiles * kmax, width), F32),
             pltpu.VMEM((cols, width), F32),
             pltpu.VMEM((2 * rows, width), F32),
+            pltpu.VMEM((2 * rows, places // 2), BF16),
         ),
         in_specs=[VMEM] * (len(near) + 2),
-        out_specs=(VMEM,) * 3,
+        out_specs=(VMEM,) * 4,
         scratch_shapes=halves,
         compiler_params=params,
         cost_estimate=pl.CostEstimate(flops=300_000_000, bytes_accessed=4_000_000, transcendentals=0),
@@ -286,7 +291,7 @@
         ],
         compiler_params=params,
         name="finish",
-    )(*[piece for piece, _ in far], panel_right, keep, *middle, inverse, left, side)
+    )(*[piece for piece, _ in far], panel_right, keep, *middle, left, side)
 
 
 def solution(mesh):

time: 29.2 us -> 29.2 us (level)
  no operation moved by 1% of the time
where the time goes in v6:
time: 29.2 us; the launch traced here: 29 us
  starting transfers between devices  13.4 us (46%)
  waiting for transfers between devices  8.65 us (30%)
  Pallas kernels  6.05 us (21%)
  between operations  0.79 us (3%)
    ppermute x12, starting transfers between devices, swap(): return lax.ppermute(block, AXIS, [(i, i ^ mask) for i in range(count)])  13.4 us
    ppermute x12, waiting for transfers between devices, swap(): return lax.ppermute(block, AXIS, [(i, i ^ mask) for i in range(count)])  8.65 us
    pallas_call x1, Pallas kernels, shards(): pl.pallas_call(functools.partial(load_kernel, kmax), out_shape=(pltpu.VME...  2.37 us
    pallas_call x1, Pallas kernels, shards(): pl.pallas_call(functools.partial(finish_kernel, [mask for _, mask in far]...  2.16 us
    pallas_call x1, Pallas kernels, shards(): pl.pallas_call(pack_kernel, out_shape=pltpu.VMEM((rows, width), F32), in_...  0.93 us
    pallas_call x1, Pallas kernels, shards(): pl.pallas_call(functools.partial(first_kernel, [mask for _, mask in near]...  0.6 us
  transfers between devices with their start and end apart: 12, of which 5 were waited for; matrix products, arithmetic and copies ran while one was open for 0% of the time, Pallas kernels for 10%

profile of v6, /device:TPU:0, one launch (start us, length us, event | category | flops | bytes accessed | tf_op | source)
XLA Modules:
  0.0 29.0 jit_solution(6540738720850339736)
XLA Ops:
  0.6 0.9 %pack.1 = f32[64,256]{1,0:T(8,128)S(1)} custom-call(bf16[64,64]{1,0:T(8,128)(2,1)} %right.1, f32[64,64]{1,0:T(8,128)} %done.1, bf16[64,64]{1,0:T(8,128)(2,1)} %left.2, f32[64,64]{1,0:T(8,128)} %side.2), custom_call_target="tpu_custom_call" | custom-call | tf_op jit(solution)/shard_map/pack/pallas_call | solution.py:231
  1.6 3.1 %collective-permute-start.7 = (f32[64,256]{1,0:T(8,128)S(1)}, f32[64,256]{1,0:T(8,128)S(1)}, u32[]{:S(2)}, u32[]{:S(2)}) collective-permute-start(f32[64,256]{1,0:T(8,128)S(1)} %pack.1), channel_id=1, source_target_pairs={{0,8},{1,9},{2,10},{3,11},{4,12},{5,13},{6,14},{7,15},{8,0},{9,1},... | collective-permute-start | bytes 196616 | tf_op jit(solution)/shard_map/ppermute | solution.py:34
  4.7 2.5 %collective-permute-start.1 = (f32[64,256]{1,0:T(8,128)S(1)}, f32[64,256]{1,0:T(8,128)S(1)}, u32[]{:S(2)}, u32[]{:S(2)}) collective-permute-start(f32[64,256]{1,0:T(8,128)S(1)} %pack.1), channel_id=1, source_target_pairs={{0,24},{1,25},{2,26},{3,27},{4,28},{5,29},{6,30},{7,31},{8,16},{9,... | collective-permute-start | bytes 196616 | tf_op jit(solution)/shard_map/ppermute | solution.py:34
  7.2 0.1 collective-permute-start
  7.3 0.0 collective-permute-done.7
  7.3 2.6 %collective-permute-start.10 = (f32[2,64,256]{2,1,0:T(8,128)S(1)}, f32[2,64,256]{2,1,0:T(8,128)S(1)}, u32[]{:S(2)}, u32[]{:S(2)}) collective-permute-start(f32[2,64,256]{2,1,0:T(8,128)S(1)} %pad_maximum_fusion.3.refs_0_), channel_id=1, source_target_pairs={{0,6},{1,7},{2,4},{3,5},{4,2},{5,3},{6,0},{7,1},{8,14},{9,15},{10,... | collective-permute-start | bytes 393224 | tf_op jit(solution)/shard_map/ppermute | solution.py:34
  9.9 0.5 %collective-permute-start.9 = (f32[2,64,256]{2,1,0:T(8,128)S(1)}, f32[2,64,256]{2,1,0:T(8,128)S(1)}, u32[]{:S(2)}, u32[]{:S(2)}) collective-permute-start(f32[2,64,256]{2,1,0:T(8,128)S(1)} %pad_maximum_fusion.3.refs_0_), channel_id=1, source_target_pairs={{0,4},{1,5},{2,6},{3,7},{4,0},{5,1},{6,2},{7,3},{8,12},{9,13},{10,... | collective-permute-start | bytes 393224 | tf_op jit(solution)/shard_map/ppermute | solution.py:34
  10.4 0.4 %collective-permute-start.8 = (f32[2,64,256]{2,1,0:T(8,128)S(1)}, f32[2,64,256]{2,1,0:T(8,128)S(1)}, u32[]{:S(2)}, u32[]{:S(2)}) collective-permute-start(f32[2,64,256]{2,1,0:T(8,128)S(1)} %pad_maximum_fusion.3.refs_0_), channel_id=1, source_target_pairs={{0,2},{1,3},{2,0},{3,1},{4,6},{5,7},{6,4},{7,5},{8,10},{9,11},{10,... | collective-permute-start | bytes 393224 | tf_op jit(solution)/shard_map/ppermute | solution.py:34
  10.8 0.7 %collective-permute-done.1 = f32[64,256]{1,0:T(8,128)S(1)} collective-permute-done((f32[64,256]{1,0:T(8,128)S(1)}, f32[64,256]{1,0:T(8,128)S(1)}, u32[]{:S(2)}, u32[]{:S(2)}) %collective-permute-start.1) | collective-permute-done | bytes 65568 | tf_op jit(solution)/shard_map/ppermute | solution.py:34
  11.5 2.1 %collective-permute-done = f32[64,256]{1,0:T(8,128)S(1)} collective-permute-done((f32[64,256]{1,0:T(8,128)S(1)}, f32[64,256]{1,0:T(8,128)S(1)}, u32[]{:S(2)}, u32[]{:S(2)}) %collective-permute-start) | collective-permute-done | bytes 65568 | tf_op jit(solution)/shard_map/ppermute | solution.py:34
  13.6 1.6 %collective-permute-start.3 = (f32[2,64,256]{2,1,0:T(8,128)S(1)}, f32[2,64,256]{2,1,0:T(8,128)S(1)}, u32[]{:S(2)}, u32[]{:S(2)}) collective-permute-start(f32[2,64,256]{2,1,0:T(8,128)S(1)} %pad_maximum_fusion.2.refs_0_), channel_id=1, source_target_pairs={{0,4},{1,5},{2,6},{3,7},{4,0},{5,1},{6,2},{7,3},{8,12},{9,13},{10,... | collective-permute-start | bytes 393224 | tf_op jit(solution)/shard_map/ppermute | solution.py:34
  15.2 1.5 %collective-permute-start.2 = (f32[2,64,256]{2,1,0:T(8,128)S(1)}, f32[2,64,256]{2,1,0:T(8,128)S(1)}, u32[]{:S(2)}, u32[]{:S(2)}) collective-permute-start(f32[2,64,256]{2,1,0:T(8,128)S(1)} %pad_maximum_fusion.2.refs_0_), channel_id=1, source_target_pairs={{0,2},{1,3},{2,0},{3,1},{4,6},{5,7},{6,4},{7,5},{8,10},{9,11},{10,... | collective-permute-start | bytes 393224 | tf_op jit(solution)/shard_map/ppermute | solution.py:34
  16.7 0.0 collective-permute-done.10.refs_3_
  16.7 0.0 collective-permute-done.9.refs_2_
  16.7 0.0 collective-permute-done.8.refs_1_
  16.8 0.1 collective-permute-start.11
  16.9 0.8 %collective-permute-start.4 = (f32[2,64,256]{2,1,0:T(8,128)S(1)}, f32[2,64,256]{2,1,0:T(8,128)S(1)}, u32[]{:S(2)}, u32[]{:S(2)}) collective-permute-start(f32[2,64,256]{2,1,0:T(8,128)S(1)} %pad_maximum_fusion.2.refs_0_), channel_id=1, source_target_pairs={{0,6},{1,7},{2,4},{3,5},{4,2},{5,3},{6,0},{7,1},{8,14},{9,15},{10,... | collective-permute-start | bytes 393224 | tf_op jit(solution)/shard_map/ppermute | solution.py:34
  17.7 1.3 %collective-permute-done.3.refs_2_ = f32[2,64,256]{2,1,0:T(8,128)S(1)} collective-permute-done((f32[2,64,256]{2,1,0:T(8,128)S(1)}, f32[2,64,256]{2,1,0:T(8,128)S(1)}, u32[]{:S(2)}, u32[]{:S(2)}) %collective-permute-start.3) | collective-permute-done | bytes 131104 | tf_op jit(solution)/shard_map/ppermute | solution.py:34
  19.1 1.6 %collective-permute-done.2.refs_1_ = f32[2,64,256]{2,1,0:T(8,128)S(1)} collective-permute-done((f32[2,64,256]{2,1,0:T(8,128)S(1)}, f32[2,64,256]{2,1,0:T(8,128)S(1)}, u32[]{:S(2)}, u32[]{:S(2)}) %collective-permute-start.2) | collective-permute-done | bytes 131104 | tf_op jit(solution)/shard_map/ppermute | solution.py:34
  20.7 0.1 collective-permute-start.6
  20.7 2.9 %collective-permute-done.4.refs_3_ = f32[2,64,256]{2,1,0:T(8,128)S(1)} collective-permute-done((f32[2,64,256]{2,1,0:T(8,128)S(1)}, f32[2,64,256]{2,1,0:T(8,128)S(1)}, u32[]{:S(2)}, u32[]{:S(2)}) %collective-permute-start.4) | collective-permute-done | bytes 131104 | tf_op jit(solution)/shard_map/ppermute | solution.py:34
  23.7 0.0 copy-start
  23.7 0.1 collective-permute-start.5
  23.8 2.4 %load.1 = (f32[128,256]{1,0:T(8,128)S(1)}, f32[64,2048]{1,0:T(8,128)S(1)}, bf16[2,64,2048]{2,1,0:T(8,128)(2,1)S(1)}, f32[2,64,2048]{2,1,0:T(8,128)S(1)}) custom-call(s32[2]{0:T(128)} %ranks.1, f32[64,2048]{1,0:T(8,128)} %inverse.1, bf16[2,64,2048]{2,1,0:T(8,128)(2,1)} %left.3, f32[2,64,2048]{2,1,0:T(8,128)} %side.3), custom_call_target="tpu_custom_call" | custom-call | tf_op jit(solution)/shard_map/load/pallas_call | solution.py:246
  26.2 0.0 collective-permute-done.11.refs_4_
  26.2 0.0 copy-done
  26.2 0.6 %first.1 = (f32[128,256]{1,0:T(8,128)S(1)}, f32[64,256]{1,0:T(8,128)S(1)}, f32[128,256]{1,0:T(8,128)S(1)}, bf16[128,1024]{1,0:T(8,128)(2,1)S(1)}) custom-call(f32[2,64,256]{2,1,0:T(8,128)S(1)} %pad_maximum_fusion.3.refs_0_, f32[2,64,256]{2,1,0:T(8,128)S(1)} %collective-permute-done.8.refs_1_, f32[2,64,256]{2,1,0:T(8,128)S(1)} %collective-permute-done.9.refs_2_, ...), custom_call_target="tpu_custom_call" | custom-call | flops 300000000 | bytes 4000000 | tf_op jit(solution)/shard_map/first/pallas_call | solution.py:261
  26.8 0.0 collective-permute-done.6.refs_5_
  26.8 0.0 collective-permute-done.5.refs_4_
  26.8 2.2 %finish.1 = (bf16[2,64,2048]{2,1,0:T(8,128)(2,1)}, f32[2,64,2048]{2,1,0:T(8,128)}, f32[64,64]{1,0:T(8,128)}) custom-call(f32[2,64,256]{2,1,0:T(8,128)S(1)} %pad_maximum_fusion.2.refs_0_, f32[2,64,256]{2,1,0:T(8,128)S(1)} %collective-permute-done.2.refs_1_, f32[2,64,256]{2,1,0:T(8,128)S(1)} %collective-permute-done.3.refs_2_, ...), custom_call_target="tpu_custom_call" | custom-call | tf_op jit(solution)/shard_map/finish/pallas_call | solution.py:276
  (9 shorter events, 0.1 us)
Async XLA Ops:
  1.6 5.7 %collective-permute-start.7 = (f32[64,256]{1,0:T(8,128)S(1)}, f32[64,256]{1,0:T(8,128)S(1)}, u32[]{:S(2)}, u32[]{:S(2)}) collective-permute-start(f32[64,256]{1,0:T(8,128)S(1)} %pack.1), channel_id=1, source_target_pairs={{0,8},{1,9},{2,10},{3,11},{4,12},{5,13},{6,14},{7,15},{8,0},{9,1},... | collective-permute-start | bytes 196616 | tf_op jit(solution)/shard_map/ppermute | solution.py:34
  4.7 6.9 %collective-permute-start.1 = (f32[64,256]{1,0:T(8,128)S(1)}, f32[64,256]{1,0:T(8,128)S(1)}, u32[]{:S(2)}, u32[]{:S(2)}) collective-permute-start(f32[64,256]{1,0:T(8,128)S(1)} %pack.1), channel_id=1, source_target_pairs={{0,24},{1,25},{2,26},{3,27},{4,28},{5,29},{6,30},{7,31},{8,16},{9,... | collective-permute-start | bytes 196616 | tf_op jit(solution)/shard_map/ppermute | solution.py:34
  7.2 6.4 %collective-permute-start = (f32[64,256]{1,0:T(8,128)S(1)}, f32[64,256]{1,0:T(8,128)S(1)}, u32[]{:S(2)}, u32[]{:S(2)}) collective-permute-start(f32[64,256]{1,0:T(8,128)S(1)} %pack.1), channel_id=1, source_target_pairs={{0,16},{1,17},{2,18},{3,19},{4,20},{5,21},{6,22},{7,23},{8,24},{9,... | collective-permute-start | bytes 196616 | tf_op jit(solution)/shard_map/ppermute | solution.py:34
  7.3 9.4 %collective-permute-start.10 = (f32[2,64,256]{2,1,0:T(8,128)S(1)}, f32[2,64,256]{2,1,0:T(8,128)S(1)}, u32[]{:S(2)}, u32[]{:S(2)}) collective-permute-start(f32[2,64,256]{2,1,0:T(8,128)S(1)} %pad_maximum_fusion.3.refs_0_), channel_id=1, source_target_pairs={{0,6},{1,7},{2,4},{3,5},{4,2},{5,3},{6,0},{7,1},{8,14},{9,15},{10,... | collective-permute-start | bytes 393224 | tf_op jit(solution)/shard_map/ppermute | solution.py:34
  9.9 6.8 %collective-permute-start.9 = (f32[2,64,256]{2,1,0:T(8,128)S(1)}, f32[2,64,256]{2,1,0:T(8,128)S(1)}, u32[]{:S(2)}, u32[]{:S(2)}) collective-permute-start(f32[2,64,256]{2,1,0:T(8,128)S(1)} %pad_maximum_fusion.3.refs_0_), channel_id=1, source_target_pairs={{0,4},{1,5},{2,6},{3,7},{4,0},{5,1},{6,2},{7,3},{8,12},{9,13},{10,... | collective-permute-start | bytes 393224 | tf_op jit(solution)/shard_map/ppermute | solution.py:34
  10.4 6.3 %collective-permute-start.8 = (f32[2,64,256]{2,1,0:T(8,128)S(1)}, f32[2,64,256]{2,1,0:T(8,128)S(1)}, u32[]{:S(2)}, u32[]{:S(2)}) collective-permute-start(f32[2,64,256]{2,1,0:T(8,128)S(1)} %pad_maximum_fusion.3.refs_0_), channel_id=1, source_target_pairs={{0,2},{1,3},{2,0},{3,1},{4,6},{5,7},{6,4},{7,5},{8,10},{9,11},{10,... | collective-permute-start | bytes 393224 | tf_op jit(solution)/shard_map/ppermute | solution.py:34
  13.6 5.4 %collective-permute-start.3 = (f32[2,64,256]{2,1,0:T(8,128)S(1)}, f32[2,64,256]{2,1,0:T(8,128)S(1)}, u32[]{:S(2)}, u32[]{:S(2)}) collective-permute-start(f32[2,64,256]{2,1,0:T(8,128)S(1)} %pad_maximum_fusion.2.refs_0_), channel_id=1, source_target_pairs={{0,4},{1,5},{2,6},{3,7},{4,0},{5,1},{6,2},{7,3},{8,12},{9,13},{10,... | collective-permute-start | bytes 393224 | tf_op jit(solution)/shard_map/ppermute | solution.py:34
  15.2 5.4 %collective-permute-start.2 = (f32[2,64,256]{2,1,0:T(8,128)S(1)}, f32[2,64,256]{2,1,0:T(8,128)S(1)}, u32[]{:S(2)}, u32[]{:S(2)}) collective-permute-start(f32[2,64,256]{2,1,0:T(8,128)S(1)} %pad_maximum_fusion.2.refs_0_), channel_id=1, source_target_pairs={{0,2},{1,3},{2,0},{3,1},{4,6},{5,7},{6,4},{7,5},{8,10},{9,11},{10,... | collective-permute-start | bytes 393224 | tf_op jit(solution)/shard_map/ppermute | solution.py:34
  16.8 9.4 %collective-permute-start.11 = (f32[8,64,256]{2,1,0:T(8,128)S(1)}, f32[8,64,256]{2,1,0:T(8,128)S(1)}, u32[]{:S(2)}, u32[]{:S(2)}) collective-permute-start(f32[8,64,256]{2,1,0:T(8,128)S(1)} %constant_dynamic-update-slice_fusion), channel_id=1, source_target_pairs={{0,1},{1,0},{2,3},{3,2},{4,5},{5,4},{6,7},{7,6},{8,9},{9,8},{10,11... | collective-permute-start | bytes 1572872 | tf_op jit(solution)/shard_map/ppermute | solution.py:34
  16.9 6.8 %collective-permute-start.4 = (f32[2,64,256]{2,1,0:T(8,128)S(1)}, f32[2,64,256]{2,1,0:T(8,128)S(1)}, u32[]{:S(2)}, u32[]{:S(2)}) collective-permute-start(f32[2,64,256]{2,1,0:T(8,128)S(1)} %pad_maximum_fusion.2.refs_0_), channel_id=1, source_target_pairs={{0,6},{1,7},{2,4},{3,5},{4,2},{5,3},{6,0},{7,1},{8,14},{9,15},{10,... | collective-permute-start | bytes 393224 | tf_op jit(solution)/shard_map/ppermute | solution.py:34
  20.7 6.1 %collective-permute-start.6 = (f32[4,64,256]{2,1,0:T(8,128)S(1)}, f32[4,64,256]{2,1,0:T(8,128)S(1)}, u32[]{:S(2)}, u32[]{:S(2)}) collective-permute-start(f32[4,64,256]{2,1,0:T(8,128)S(1)} %pad_maximum_fusion.1), channel_id=1, source_target_pairs={{0,1},{1,0},{2,3},{3,2},{4,5},{5,4},{6,7},{7,6},{8,9},{9,8},{10,11... | collective-permute-start | bytes 786440 | tf_op jit(solution)/shard_map/ppermute | solution.py:34
  23.7 2.5 %copy-start = (bf16[2,64,2048]{2,1,0:T(8,128)(2,1)S(1)}, bf16[2,64,2048]{2,1,0:T(8,128)(2,1)}, u32[]{:S(2)}) copy-start(bf16[2,64,2048]{2,1,0:T(8,128)(2,1)} %refs_6_.1) | copy-start | bytes 1572868
  23.7 3.1 %collective-permute-start.5 = (f32[4,64,256]{2,1,0:T(8,128)S(1)}, f32[4,64,256]{2,1,0:T(8,128)S(1)}, u32[]{:S(2)}, u32[]{:S(2)}) collective-permute-start(f32[4,64,256]{2,1,0:T(8,128)S(1)} %pad_maximum_fusion), channel_id=1, source_target_pairs={{0,1},{1,0},{2,3},{3,2},{4,5},{5,4},{6,7},{7,6},{8,9},{9,8},{10,11... | collective-permute-start | bytes 786440 | tf_op jit(solution)/shard_map/ppermute | solution.py:34
